TPU v7x, 128 devices: a whole 4x4x4 slice. The times are simulated.
128 devices in a mesh: dp: 16 (over x_hi, z, core), tensor: 8 (over x_lo, y).
Axes of the slice: x: 4 (x_hi: 2, x_lo: 2; x = x_hi * 2 + x_lo), y: 4, z: 4, core: 2. Of those that a mesh axis runs over, the one named last changes fastest.
Arguments:
- tokens: bfloat16 [20480, 4096], P(('dp', 'tensor')), parts along dimension 0, may hold values from -6 to 6
- norm_gain: bfloat16 [4096], replicated, may hold values from 0.099609375 to 1.8984375
- query_weight: bfloat16 [4096, 8192], P(None, 'tensor'), may hold values from -0.09375 to 0.09375
- key_weight: bfloat16 [4096, 1024], P(None, 'tensor'), may hold values from -0.09375 to 0.09375
- value_weight: bfloat16 [4096, 1024], P(None, 'tensor'), may hold values from -0.09375 to 0.09375
- out_weight: bfloat16 [8192, 4096], P('tensor'), may hold values from -0.0625 to 0.0625
- past_cache: bfloat16 [2048, 64, 2, 1024], P('dp', None, None, 'tensor'), parts along dimension 0, may hold values from -320 to 320
- exponents: int32 [20480, 32], P('dp'), parts along dimension 0, may hold values from -11 to -7
Outputs:
- mixed: bfloat16 [20480, 4096], P(('dp', 'tensor')), parts along dimension 0
There are 16 independent parts, one for each index of `dp`. A program takes and returns all parts, laid end to end along the dimension named above; an argument that names none is the same for every part. Nothing has to cross between parts.
All inputs are finite; a program needn't handle non-finite values.
Results may differ from a plain program's by a relative error of at most 0.012.
The roundings to bfloat16 on the way count: a program that leaves them out, or rounds other values in their place, can miss the bound.
Values may be sent and summed in bfloat16 or wider, within the bound.
A program may use at most 192 MiB of HBM per device.

v0:
```python
import jax
import jax.numpy as jnp
from jax import lax
from jax.sharding import PartitionSpec as P

HD = 128
NEW = 10
CACHE = 64


epsilon = 1e-05
theta_base = 500000.0


def in_order(pieces, dim):
    pieces = jnp.moveaxis(pieces, 0, dim)
    dims = pieces.shape
    return pieces.reshape(*dims[:dim], dims[dim] * dims[dim + 1], *dims[dim + 2 :])


def work_in_pieces(x, axis, dim, apply, out_dim):
    size, width = (lax.axis_size(axis), x.shape[dim])
    count = 2 if width % 2 == 0 else 1
    finished, length = ([], width // count)
    for k in range(count):
        share = lax.slice_in_dim(x, k * length, (k + 1) * length, axis=dim)
        starts = jnp.arange(size) * width + k * length
        finished.append(jax.vmap(apply)(lax.all_gather(share, axis), starts))
    return in_order(jnp.concatenate(finished, axis=out_dim + 1), out_dim)


def rotate(matrix, heads):
    row_count = matrix.shape[0]
    half_dim = HD // 2
    positions = (jnp.arange(row_count, dtype=jnp.int32) % NEW + CACHE).astype(jnp.float32)
    frequency = theta_base ** (-(jnp.arange(half_dim, dtype=jnp.float32) * 2.0) / HD)
    angles = positions[:, None] * frequency[None, :]
    cosine = jnp.cos(angles)[:, None, :]
    sine_part = jnp.sin(angles)[:, None, :]
    shaped = matrix.reshape(row_count, heads, 2, half_dim)
    first = shaped[:, :, 0]
    second = shaped[:, :, 1]
    turned = jnp.stack(
        [first * cosine - second * sine_part, second * cosine + first * sine_part], 2
    )
    return turned.reshape(row_count, heads * HD)


def attention(query, key_new, value_new, past_cache, kv_heads):
    row_count = query.shape[0]
    seq_count = row_count // NEW
    group_size = query.shape[1] // (kv_heads * HD)
    cache_len = past_cache.shape[1]
    query_heads = query.reshape(seq_count, NEW, kv_heads, group_size, HD)
    new_keys = key_new.reshape(seq_count, NEW, kv_heads, HD)
    new_values = value_new.reshape(seq_count, NEW, kv_heads, HD)
    cache_keys = past_cache[:, :, 0].reshape(seq_count, cache_len, kv_heads, HD)
    cache_values = past_cache[:, :, 1].reshape(seq_count, cache_len, kv_heads, HD)
    inv_root = 1.0 / HD**0.5
    cache_scores = (
        jnp.einsum("stkgd,sckd->skgtc", query_heads, cache_keys, preferred_element_type=jnp.float32)
        * inv_root
    )
    new_scores = (
        jnp.einsum("stkgd,sukd->skgtu", query_heads, new_keys, preferred_element_type=jnp.float32)
        * inv_root
    )
    causal = jnp.arange(NEW)[:, None] >= jnp.arange(NEW)[None, :]
    new_scores = jnp.where(causal, new_scores, -1e30)
    row_max = jnp.maximum(cache_scores.max(-1), new_scores.max(-1))[..., None]
    cache_probs = jnp.exp(cache_scores - row_max)
    new_probs = jnp.exp(new_scores - row_max)
    denominator = (cache_probs.sum(-1) + new_probs.sum(-1))[..., None]
    cache_weights = (cache_probs / denominator).astype(jnp.bfloat16)
    new_weights = (new_probs / denominator).astype(jnp.bfloat16)
    combined = jnp.einsum(
        "skgtc,sckd->stkgd", cache_weights, cache_values, preferred_element_type=jnp.float32
    )
    combined = combined + jnp.einsum(
        "skgtu,sukd->stkgd", new_weights, new_values, preferred_element_type=jnp.float32
    )
    return combined.reshape(row_count, kv_heads * group_size * HD).astype(jnp.bfloat16)


def on_device(
    tokens, norm_gain, query_weight, key_weight, value_weight, out_weight, past_cache, exponents
):
    kv_local = key_weight.shape[1] // HD
    query_local = query_weight.shape[1] // HD
    query_cols = query_weight.shape[1]
    key_cols = key_weight.shape[1]
    gain_f32 = norm_gain.astype(jnp.float32)

    def project(block_rows, offset):
        floats = block_rows.astype(jnp.float32)
        normed = floats * lax.rsqrt(jnp.mean(floats * floats, axis=-1, keepdims=True) + epsilon)
        normed = (normed * gain_f32).astype(jnp.bfloat16)
        return jnp.concatenate(
            [
                jnp.dot(normed, query_weight, preferred_element_type=jnp.float32),
                jnp.dot(normed, key_weight, preferred_element_type=jnp.float32),
                jnp.dot(normed, value_weight, preferred_element_type=jnp.float32),
            ],
            1,
        )

    projected = work_in_pieces(tokens, "tensor", 0, project, 0)
    query = rotate(projected[:, :query_cols], query_local).astype(jnp.bfloat16)
    key_new = rotate(projected[:, query_cols : query_cols + key_cols], kv_local).astype(
        jnp.bfloat16
    )
    value_new = projected[:, query_cols + key_cols :].astype(jnp.bfloat16)
    attended = attention(query, key_new, value_new, past_cache, kv_local)
    partial_value = jnp.dot(attended, out_weight, preferred_element_type=jnp.float32)
    row_count = partial_value.shape[0]
    groups = exponents.shape[1]
    shrink = jnp.exp2(-exponents.astype(jnp.float32))[..., None]
    scaled = jnp.clip(partial_value.reshape(row_count, groups, -1) * shrink, -127.0, 127.0)
    rounded = lax.optimization_barrier(scaled.astype(jnp.bfloat16)).astype(jnp.float32)
    rounded = rounded.reshape(row_count, -1)
    own_rows = row_count // lax.axis_size("tensor")
    share = lax.psum_scatter(
        rounded.astype(jnp.bfloat16), "tensor", scatter_dimension=0, tiled=True
    ).astype(jnp.float32)
    own_exponents = lax.dynamic_slice_in_dim(
        exponents, lax.axis_index("tensor") * own_rows, own_rows, 0
    )
    restore = jnp.exp2(own_exponents.astype(jnp.float32))[..., None]
    layer_out = tokens.astype(jnp.float32) + (
        share.reshape(own_rows, groups, -1) * restore
    ).reshape(own_rows, -1)
    return layer_out.astype(jnp.bfloat16)


def solution(mesh):
    return jax.shard_map(
        on_device,
        mesh=mesh,
        in_specs=(
            P(("dp", "tensor"), None),
            P(),
            P(None, "tensor"),
            P(None, "tensor"),
            P(None, "tensor"),
            P("tensor", None),
            P("dp", None, None, "tensor"),
            P("dp", None),
        ),
        out_specs=P(("dp", "tensor"), None),
        check_vma=False,
    )
```

profile of v0, /device:TPU:0, one launch (start us, length us, event | category | flops | bytes accessed | tf_op | source)
XLA Modules:
  0.0 434.6 jit_solution(7827488118867053869)
XLA Ops:
  6.5 2.6 fusion.66
  10.6 12.0 %copy.95 = bf16[4096,1024]{1,0:T(8,128)(2,1)} copy(bf16[4096,1024]{0,1:T(8,128)(2,1)} %bitcast.113) | data formatting | bytes 16777216 | tf_op jit(solution)/shard_map/dot_general | solution.py:114
  24.6 15.5 %fusion.65 = (bf16[128,64,1,128]{3,2,1,0:T(2,128)(2,1)}, bf16[128,64,1,128]{3,2,1,0:T(2,128)(2,1)}) fusion(bf16[128,64,2,128]{3,2,1,0:T(2,128)(2,1)} %param.14), kind=kLoop, calls=%fused_computation.90 | loop fusion | bytes 8388608 | tf_op jit(solution)/shard_map/slice | solution.py:58
  40.2 34.0 %all-gather.5.cloned.1.call-done = bf16[640,4096]{1,0:T(8,128)(2,1)} async-done(((bf16[80,4096]{1,0:T(8,128)(2,1)}), bf16[640,4096]{1,0:T(8,128)(2,1)}) %all-gather.5.cloned.1.call-update) | async-done | bytes 5242896 | tf_op jit(solution)/shard_map/all_gather | solution.py:28
  74.1 3.6 fusion.2
  77.7 59.2 %all-gather.7.cloned.1.call-done = bf16[640,4096]{1,0:T(8,128)(2,1)} async-done(((bf16[80,4096]{1,0:T(8,128)(2,1)}), bf16[640,4096]{1,0:T(8,128)(2,1)}) %all-gather.7.cloned.1.call-update) | async-done | bytes 5242896 | tf_op jit(solution)/shard_map/all_gather | solution.py:28
  136.9 3.7 fusion.5
  141.0 9.4 %fusion.11 = f32[8,80,1024]{2,1,0:T(8,128)S(1)} fusion(bf16[4096,1024]{1,0:T(8,128)(2,1)} %param.10, bf16[8,80,4096]{2,1,0:T(8,128)(2,1)S(1)} %bitcast.116, f32[4096]{0:T(1024)S(1)} %convert_element_type.94, f32[8,80]{1,0:T(8,128)S(1)} %add_rsqrt_fusion.1), kind=kOutput, calls=%fused_computation.18 | convolution fusion | flops 5379194880 | bytes 16271872 | tf_op jit(solution)/shard_map/vmap()/dot_general | solution.py:100
  150.4 5.7 %fusion.9 = f32[8,80,1024]{2,1,0:T(8,128)S(1)} fusion(bf16[4096,1024]{1,0:T(8,128)(2,1)S(1)} %bitcast.127, bf16[8,80,4096]{2,1,0:T(8,128)(2,1)S(1)} %bitcast.122, f32[8,80]{1,0:T(8,128)S(1)} %add_rsqrt_fusion, f32[4096]{0:T(1024)S(1)} %convert_element_type.94), kind=kOutput, calls=%fused_computation.16 | convolution fusion | flops 5379194880 | bytes 16271872 | tf_op jit(solution)/shard_map/vmap()/dot_general | solution.py:100
  156.1 1.6 fusion.28
  157.7 1.6 fusion.33
  160.9 1.6 fusion.35
  163.2 3.4 slice.45
  167.6 5.9 %copy.98 = f32[1280,1024]{0,1:T(8,128)} copy(f32[1280,1024]{1,0:T(8,128)} %slice.45) | data formatting | bytes 10485760
  173.5 3.2 subtract_convert_fusion
  176.8 1.7 pad_maximum_fusion
  178.5 11.7 %copy.69 = bf16[1280,8,2,64]{3,2,1,0:T(2,128)(2,1)} copy(bf16[1280,8,2,64]{0,3,2,1:T(8,128)(2,1)} %pad_maximum_fusion) | data formatting | bytes 5242880 | tf_op jit(solution)/shard_map/stack | solution.py:43
  190.2 9.3 %convert_element_type.99 = bf16[128,10,8,128]{3,2,1,0:T(8,128)(2,1)} reshape(bf16[1280,8,2,64]{3,2,1,0:T(2,128)(2,1)} %copy.69) | data formatting | bytes 5242880 | tf_op jit(solution)/shard_map/convert_element_type | solution.py:108
  199.5 6.8 %bitcast_reduce_fusion = (f32[128,8,10]{1,2,0:T(8,128)S(1)}, f32[128,10,8,64]{3,2,1,0:T(8,128)}) fusion(bf16[128,10,8,128]{3,2,1,0:T(8,128)(2,1)} %convert_element_type.99, bf16[128,64,1,128]{3,2,1,0:T(2,128)(2,1)} %get-tuple-element.8), kind=kOutput, calls=%fused_computation.26 | convolution fusion | flops 169072640 | bytes 7380992 | tf_op jit(solution)/shard_map/stkgd,sckd->skgtc/dot_general | solution.py:61
  209.2 15.0 %fusion.14 = (f32[128,8,10]{2,1,0:T(8,128)S(1)}, f32[128,10,10,8]{2,1,3,0:T(8,128)}) fusion(pred[10,10]{0,1:T(8,128)(4,1)S(1)} %iota_compare_fusion, bf16[128,10,8,128]{3,2,1,0:T(8,128)(2,1)} %convert_element_type.99, bf16[128,10,128,1]{2,1,0,3:T(8,128)(2,1)S(1)} %reshape.280), kind=kOutput, calls=%fused_computation.24 | convolution fusion | flops 26511360 | bytes 3399780 | tf_op jit(solution)/shard_map/stkgd,sukd->skgtu/dot_general | solution.py:65
  225.1 5.4 %fusion.13 = f32[128,8,10]{2,1,0:T(8,128)S(1)} fusion(f32[128,10,10,8]{2,1,3,0:T(8,128)} %get-tuple-element.18, f32[128,8,10]{2,1,0:T(8,128)S(1)} %copy.77, pred[10,10]{0,1:T(8,128)(4,1)S(1)} %iota_compare_fusion), kind=kLoop, calls=%fused_computation.22 | loop fusion | flops 399360 | bytes 491620 | tf_op jit(solution)/shard_map/reduce_sum | solution.py:73
  230.8 5.8 %fusion.16 = f32[128,8,10]{1,2,0:T(8,128)S(1)} fusion(f32[128,10,8,64]{3,2,1,0:T(8,128)} %get-tuple-element.16, f32[128,8,10]{1,2,0:T(8,128)S(1)} %copy.76), kind=kLoop, calls=%fused_computation.29 | loop fusion | flops 1955840 | bytes 2703360 | tf_op jit(solution)/shard_map/reduce_sum | solution.py:73
  238.8 7.3 %fusion.42 = bf16[128,8,10,64]{3,1,2,0:T(8,128)(2,1)} fusion(f32[128,8,10]{1,2,0:T(8,128)S(1)} %copy.80, f32[128,8,10]{1,2,0:T(8,128)S(1)} %copy.76, f32[128,10,8,64]{3,2,1,0:T(8,128)} %get-tuple-element.16), kind=kLoop, calls=%fused_computation.49 | loop fusion | flops 2621440 | bytes 4014080 | tf_op jit(solution)/shard_map/reshape.10
  246.3 7.2 %fusion.18 = f32[128,128,8,10]{1,3,2,0:T(8,128)} fusion(f32[128,10,10,8]{2,1,3,0:T(8,128)} %get-tuple-element.18, f32[128,8,10]{2,1,0:T(8,128)S(1)} %copy.83, f32[128,8,10]{2,1,0:T(8,128)S(1)} %copy.77, pred[10,10]{0,1:T(8,128)(4,1)S(1)} %iota_compare_fusion, bf16[128,10,128,1]{2,1,0,3:T(8,128)(2,1)S(1)} %reshape.282), kind=kOutput, calls=%fused_computation.31 | convolution fusion | flops 26726400 | bytes 6062180 | tf_op jit(solution)/shard_map/skgtu,sukd->stkgd/dot_general | solution.py:79
  253.5 4.8 %fusion.17 = bf16[128,10,1,8,128]{4,1,3,0,2:T(8,128)(2,1)S(1)} fusion(f32[128,128,8,10]{1,3,2,0:T(8,128)} %fusion.18, bf16[128,8,10,64]{3,1,2,0:T(8,128)(2,1)S(1)} %copy-done.3, bf16[128,64,1,128]{3,2,1,0:T(2,128)(2,1)S(1)} %copy-done.4), kind=kOutput, calls=%fused_computation.30 | convolution fusion | flops 170393600 | bytes 11272192 | tf_op jit(solution)/shard_map/skgtc,sckd->stkgd/dot_general | solution.py:76
  258.4 2.9 copy.85
  261.3 5.2 %reshape.283 = bf16[1280,1024,1]{1,0,2:T(8,128)(2,1)} reshape(bf16[128,10,1,8,128]{4,3,1,0,2:T(8,128)(2,1)} %copy.85) | data formatting | bytes 5242880 | tf_op jit(solution)/shard_map/convert_element_type | solution.py:82
  266.5 16.1 %fusion.1 = bf16[1280,32,128]{2,0,1:T(8,128)(2,1)} fusion(bf16[1280,1024,1]{1,0,2:T(8,128)(2,1)} %reshape.283, bf16[32,128,1024]{2,1,0:T(8,128)(2,1)} %bitcast.114, f32[1280,32]{0,1:T(8,128)S(1)} %copy-done.8), kind=kOutput, calls=%fused_computation.2 | convolution fusion | flops 10753146880 | bytes 21659648 | tf_op jit(solution)/shard_map/dot_general | solution.py:114
  282.6 14.4 %copy.87 = bf16[1280,32,128]{0,2,1:T(8,128)(2,1)} copy(bf16[1280,32,128]{2,0,1:T(8,128)(2,1)} %fusion.1) | data formatting | bytes 20971520 | tf_op jit(solution)/shard_map/optimization_barrier | solution.py:119
  297.0 14.3 %copy.96 = bf16[1280,4096]{1,0:T(8,128)(2,1)} copy(bf16[1280,4096]{0,1:T(8,128)(2,1)} %bitcast.107) | data formatting | bytes 20971520
  312.5 110.3 %reduce-scatter.4.cloned.1.call-done = bf16[160,4096]{1,0:T(8,128)(2,1)} async-done(((bf16[1280,4096]{1,0:T(8,128)(2,1)}), bf16[160,4096]{1,0:T(8,128)(2,1)}) %reduce-scatter.4.cloned.1.call-update) | async-done | bytes 1310736 | tf_op jit(solution)/shard_map/reduce_scatter | solution.py:122
  423.5 4.3 fusion.41
  (67 shorter events, 15.1 us)
Async XLA Ops:
  6.5 149.6 %copy-start = (bf16[4096,128]{1,0:T(8,128)(2,1)S(1)}, bf16[4096,128]{1,0:T(8,128)(2,1)}, u32[]{:S(2)}) copy-start(bf16[4096,128]{1,0:T(8,128)(2,1)} %param.12) | copy-start | bytes 3145732
  6.5 67.6 %all-gather.5.cloned.1.call-start = ((), (), s32[]{:S(2)}) async-start(), calls=%async_computation.1 | async-start | bytes 5898240 | tf_op jit(solution)/shard_map/all_gather | solution.py:28
  9.1 127.8 %all-gather.7.cloned.1.call-start = ((), (), s32[]{:S(2)}) async-start(), calls=%async_computation.2 | async-start | bytes 5898240 | tf_op jit(solution)/shard_map/all_gather | solution.py:28
  9.9 412.9 %reduce-scatter.4.cloned.1.call-start = ((), (), s32[]{:S(2)}) async-start(), calls=%async_computation.3 | async-start | bytes 11796480 | tf_op jit(solution)/shard_map/reduce_scatter | solution.py:122
  10.6 12.1 %copy-start.7 = (s32[1280,32]{0,1:T(8,128)S(1)}, s32[1280,32]{0,1:T(8,128)}, u32[]{:S(2)}) copy-start(s32[1280,32]{0,1:T(8,128)} %param.15) | copy-start | bytes 491524
  136.9 4.0 copy-start.5
  136.9 13.5 %slice-start = ((s8[5242880]{0:T(1024)(128)(4,1)}), s8[4194304]{0:T(1024)(128)(4,1)S(1)}, s32[]{:S(2)}) async-start(s8[5242880]{0:T(1024)(128)(4,1)} %bitcast.120), calls=%async_computation.4 | async-start | bytes 8388608
  136.9 13.5 %slice-start.2 = ((s8[8388608]{0:T(1024)(128)(4,1)}), s8[4194304]{0:T(1024)(128)(4,1)S(1)}, s32[]{:S(2)}) async-start(s8[8388608]{0:T(1024)(128)(4,1)} %bitcast.126), calls=%async_computation.6 | async-start | bytes 8388608
  141.0 9.4 %slice-start.1 = ((s8[5242880]{0:T(1024)(128)(4,1)}), s8[1048576]{0:T(1024)(128)(4,1)S(1)}, s32[]{:S(2)}) async-start(s8[5242880]{0:T(1024)(128)(4,1)} %bitcast.120), calls=%async_computation.5 | async-start | bytes 2097152
  141.0 9.4 %slice-start.3 = ((s8[8388608]{0:T(1024)(128)(4,1)}), s8[4194304]{0:T(1024)(128)(4,1)S(1)}, s32[]{:S(2)}) async-start(s8[8388608]{0:T(1024)(128)(4,1)} %bitcast.126), calls=%async_computation.7 | async-start | bytes 8388608
  157.7 1.6 copy-start.9
  163.2 4.4 %copy-start.2 = (f32[8,160,1280]{2,1,0:T(8,128)}, f32[8,160,1280]{2,1,0:T(8,128)S(1)}, u32[]{:S(2)}) copy-start(f32[8,160,1280]{2,1,0:T(8,128)S(1)} %maximum_maximum_fusion) | copy-start | bytes 19660804
  246.3 7.2 %copy-start.3 = (bf16[128,8,10,64]{3,1,2,0:T(8,128)(2,1)S(1)}, bf16[128,8,10,64]{3,1,2,0:T(8,128)(2,1)}, u32[]{:S(2)}) copy-start(bf16[128,8,10,64]{3,1,2,0:T(8,128)(2,1)} %fusion.42) | copy-start | bytes 3932164
  246.3 7.2 %copy-start.4 = (bf16[128,64,1,128]{3,2,1,0:T(2,128)(2,1)S(1)}, bf16[128,64,1,128]{3,2,1,0:T(2,128)(2,1)}, u32[]{:S(2)}) copy-start(bf16[128,64,1,128]{3,2,1,0:T(2,128)(2,1)} %get-tuple-element.7) | copy-start | bytes 6291460
  258.4 8.1 %copy-start.8 = (f32[1280,32]{0,1:T(8,128)S(1)}, f32[1280,32]{0,1:T(8,128)}, u32[]{:S(2)}) copy-start(f32[1280,32]{0,1:T(8,128)} %multiply_exponential_fusion) | copy-start | bytes 491524
  311.3 112.2 %copy-start.6 = (bf16[160,4096]{1,0:T(8,128)(2,1)S(1)}, bf16[160,4096]{1,0:T(8,128)(2,1)}, u32[]{:S(2)}) copy-start(bf16[160,4096]{1,0:T(8,128)(2,1)} %param.8) | copy-start | bytes 3932164
  311.3 116.5 %copy-start.1 = (bf16[4096,128]{1,0:T(8,128)(2,1)S(1)}, bf16[4096,128]{1,0:T(8,128)(2,1)}, u32[]{:S(2)}) copy-start(bf16[4096,128]{1,0:T(8,128)(2,1)} %param.12) | copy-start | bytes 3145732
Sparse Core Ops, SparseCore 0:
  9.2 64.8 all-gather.4
  75.8 61.1 all-gather.6
  311.4 111.2 reduce-scatter.3
where the time goes:
time: 443 us; the launch traced here: 435 us
  waiting for transfers between devices  204 us (46%)
  local copies, waits for them, and re-layouts  104 us (23%)
  matrix products  71.4 us (16%)
  other arithmetic  41 us (9%)
  between operations  13.7 us (3%)
    reduce_scatter x1, waiting for transfers between devices, on_device(): lax.psum_scatter(rounded.astype(jnp.bfloat16), 'tensor', scatter_dimensio...  110 us
    all_gather x2, waiting for transfers between devices, work_in_pieces(): finished.append(jax.vmap(apply)(lax.all_gather(share, axis), starts))  93.2 us
    unnamed x31, local copies, waits for them, and re-layouts  21.8 us
    dot_general x1, matrix products, on_device(): jnp.dot(attended, out_weight, preferred_element_type=jnp.float32)  16.1 us
    slice x1, local copies, waits for them, and re-layouts, attention(): past_cache[:, :, 1].reshape(seq_count, cache_len, kv_heads, HD)  15.5 us
    dot_general x2, matrix products, project(): jnp.dot(normed, query_weight, preferred_element_type=jnp.float32)  15.1 us
    dot_general x1, matrix products, attention(): jnp.einsum('stkgd,sukd->skgtu', query_heads, new_keys, preferred_element_...  15 us
    optimization_barrier x1, local copies, waits for them, and re-layouts, on_device(): lax.optimization_barrier(scaled.astype(jnp.bfloat16)).astype(jnp.float32)  14.4 us
  transfers between devices with their start and end apart: 3, of which 3 were waited for; matrix products, arithmetic and copies ran while one was open for 8% of the time, Pallas kernels for 0%

commit v1 on v0

v1 whole, which is shorter than its diff:
```python
import functools

import jax
import jax.numpy as jnp
import numpy as np
from jax import lax
from jax.experimental import pallas as pl
from jax.experimental.pallas import tpu as pltpu
from jax.sharding import PartitionSpec as P

HD = 128
NEW = 10
CACHE = 64
D = 4096
HEADS = 8
QC = 1024
SEQ_BLOCK = 16
ROWS_B = 160
PADDED = 256
CH = 1024
NQ = 4
EPS = 1e-05
THETA = 500000.0
MESH = pl.DeviceIdType.MESH
F32 = jnp.float32
BF16 = jnp.bfloat16

SLOTS = ((0, 0), (0, 3), (0, 1), (1, 0), (0, 2), (1, 2), (1, 3), (1, 1))
DX_BITS = sum(dx << j for j, (dx, _) in enumerate(SLOTS))
DY_BITS = sum(dy << (2 * j) for j, (_, dy) in enumerate(SLOTS))

UP, DOWN, ACROSS = "up", "down", "across"
GATHER = {
    "own_up": (UP, "x", 0, "x", 1, (0, 1, 2, 3)),
    "own_down": (DOWN, "x", 0, "x", 2, (2, 3, 0, 1)),
    "own_across": (ACROSS, "x", 0, "x", 3, (0, 1, 2, 3)),
    "far_up": (UP, "x", 1, "x", 4, (0, 1)),
    "far_down": (DOWN, "x", 2, "x", 4, (2, 3)),
    "far_across": (ACROSS, "x", 4, "x", 5, (0, 2, 1, 3)),
    "side_up": (UP, "x", 3, "x", 6, (0, 1, 2, 3)),
    "side_down": (DOWN, "x", 3, "x", 7, (0, 1, 2, 3)),
}
R_FAR, R_HALF, R_SIDE_P, R_SIDE_M, R_P, R_M, R_X = range(7)
SCATTER = {
    "r_far": (ACROSS, "p", 5, "r", R_FAR, (0, 2, 1, 3)),
    "r_half_down": (DOWN, "p", 4, "r", R_HALF, (0, 1)),
    "r_half_up": (UP, "p", 4, "r", R_HALF, (2, 3)),
    "r_near_down": (DOWN, "p", 1, "r", R_P, (2, 3, 0, 1)),
    "r_near_up": (UP, "p", 2, "r", R_M, (0, 1, 2, 3)),
    "r_side_down": (DOWN, "p", 6, "r", R_SIDE_P, (0, 1, 2, 3)),
    "r_side_up": (UP, "p", 7, "r", R_SIDE_M, (0, 1, 2, 3)),
    "r_across": (ACROSS, "p", 3, "r", R_X, (0, 1, 2, 3)),
}
ROUTES = {**GATHER, **SCATTER}
ROUTE_ID = {name: i for i, name in enumerate(ROUTES)}


def body(
    tokens_hbm, gain_ref, wq_hbm, wk_hbm, wv_hbm, wo_hbm, kv_hbm, exps_ref, cos_ref, sin_ref,
    pad_ref, unpad_ref, out_hbm,
    xg, pb, rb, w_in, w_out, kv, xn, qp, ap, ab, obuf,
    load_sem, send_sem, recv_sem, out_sem,
):
    me = lax.axis_index("tensor")
    mx, my = me // 4, me % 4
    targets = {
        UP: mx * 4 + (my + 1) % 4,
        DOWN: mx * 4 + (my + 3) % 4,
        ACROSS: (1 - mx) * 4 + my,
    }
    buffers = {"x": xg, "p": pb, "r": rb}

    def cols(q):
        return pl.ds(q * CH, CH)

    def route(name, q):
        link, sbuf, sslot, dbuf, dslot, _ = ROUTES[name]
        k = ROUTE_ID[name] * NQ + q
        return pltpu.make_async_remote_copy(
            src_ref=buffers[sbuf].at[sslot, :, cols(q)],
            dst_ref=buffers[dbuf].at[dslot, :, cols(q)],
            send_sem=send_sem.at[k],
            recv_sem=recv_sem.at[k],
            device_id={"tensor": targets[link]},
            device_id_type=MESH,
        )

    def send(name, quarters=None):
        for q in quarters if quarters is not None else ROUTES[name][5]:
            route(name, q).start()

    def arrived(name, quarters=None):
        for q in quarters if quarters is not None else ROUTES[name][5]:
            route(name, q).wait_recv()

    own = [
        pltpu.make_async_copy(tokens_hbm.at[:, cols(q)], xg.at[0, :, cols(q)], load_sem.at[q])
        for q in range(NQ)
    ]
    load_q = pltpu.make_async_copy(wq_hbm, w_in.at[:, pl.ds(0, QC)], load_sem.at[4])
    load_k = pltpu.make_async_copy(wk_hbm, w_in.at[:, pl.ds(QC, HD)], load_sem.at[5])
    load_v = pltpu.make_async_copy(wv_hbm, w_in.at[:, pl.ds(QC + HD, HD)], load_sem.at[6])
    load_kv = pltpu.make_async_copy(kv_hbm, kv, load_sem.at[7])
    load_o = pltpu.make_async_copy(wo_hbm, w_out, load_sem.at[8])
    for copy in (*own, load_q, load_k, load_v, load_kv, load_o):
        copy.start()

    barrier = pltpu.get_barrier_semaphore()
    for link in (UP, DOWN, ACROSS):
        pl.semaphore_signal(barrier, inc=1, device_id={"tensor": targets[link]}, device_id_type=MESH)
    pl.semaphore_wait(barrier, 3)

    for copy in own:
        copy.wait()
    for i in range(NQ):
        for name in ("own_up", "own_down", "own_across"):
            route(name, ROUTES[name][5][i]).start()

    def norm(j):
        def tile(i, c):
            rows = pl.ds(pl.multiple_of(i * 16, 16), 16)
            x = xg[j, rows, :].astype(F32)
            scale = lax.rsqrt(jnp.mean(x * x, axis=-1, keepdims=True) + EPS)
            xn[rows, :] = (x * scale * gain_ref[...].astype(F32)).astype(BF16)
            return c

        lax.fori_loop(0, ROWS_B // 16, tile, 0)

    def rot(m):
        return m * cos_ref[...] + pltpu.roll(m, HD // 2, 1) * sin_ref[...]

    def project():
        def tile(n, c):
            at = pl.ds(pl.multiple_of(n * 256, 256), 256)
            m = jnp.dot(xn[...], w_in[:, at], preferred_element_type=F32)
            turned = jnp.concatenate([rot(m[:, :HD]), rot(m[:, HD:])], 1).astype(BF16)
            qp[:, at] = jnp.dot(pad_ref[...], turned, preferred_element_type=F32).astype(BF16)
            return c

        lax.fori_loop(0, 4, tile, 0)
        m = jnp.dot(xn[...], w_in[:, QC:], preferred_element_type=F32)
        turned = jnp.concatenate([rot(m[:, :HD]), m[:, HD:]], 1).astype(BF16)
        qp[:, QC:] = jnp.dot(pad_ref[...], turned, preferred_element_type=F32).astype(BF16)

    def attend(t):
        inv_root = 1.0 / HD**0.5
        lane = lax.broadcasted_iota(jnp.int32, (HD, 2 * CACHE), 1)
        is_key = lane % 2 == 0
        new_row = lax.broadcasted_iota(jnp.int32, (HD, 16), 0) % 16
        new_lane = lax.broadcasted_iota(jnp.int32, (HD, 16), 1)
        seen = new_lane <= new_row
        contract_last = (((1,), (1,)), ((), ()))

        def seq(s, c):
            rows = pl.ds(pl.multiple_of(s * 16, 16), 16)
            query = jnp.concatenate([qp[rows, h * HD : (h + 1) * HD] for h in range(HEADS)], 0)
            key_new = qp[rows, QC : QC + HD]
            value_new = qp[rows, QC + HD :]
            pairs = kv[t * SEQ_BLOCK + s]
            s_old = lax.dot_general(query, pairs, contract_last, preferred_element_type=F32)
            s_new = lax.dot_general(query, key_new, contract_last, preferred_element_type=F32)
            s_old = jnp.where(is_key, s_old * inv_root, -1e30)
            s_new = jnp.where(seen, s_new * inv_root, -1e30)
            top = jnp.maximum(
                jnp.max(s_old, axis=1, keepdims=True), jnp.max(s_new, axis=1, keepdims=True)
            )
            e_old = jnp.exp(s_old - top)
            e_new = jnp.exp(s_new - top)
            total = jnp.sum(e_old, axis=1, keepdims=True) + jnp.sum(e_new, axis=1, keepdims=True)
            inverse = 1.0 / total
            p_old = pltpu.roll(e_old * inverse, 1, 1).astype(BF16)
            p_new = (e_new * inverse).astype(BF16)
            att = jnp.dot(p_old, pairs, preferred_element_type=F32)
            att = (att + jnp.dot(p_new, value_new, preferred_element_type=F32)).astype(BF16)
            for h in range(HEADS):
                ap[rows, h * HD : (h + 1) * HD] = att[h * 16 : (h + 1) * 16]
            return c

        lax.fori_loop(0, SEQ_BLOCK, seq, 0, unroll=2)
        for n in range(4):
            at = slice(n * 256, (n + 1) * 256)
            ab[:, at] = jnp.dot(
                unpad_ref[...], ap[:, at], preferred_element_type=F32
            ).astype(BF16)

    def powers(t, sign):
        e = exps_ref[pl.ds(pl.multiple_of(t * ROWS_B, ROWS_B), ROWS_B), :]
        if sign < 0:
            return jnp.left_shift(1, -e).astype(F32)
        return jnp.left_shift(1, e + 11).astype(F32) * (2.0**-11)

    def out_project(j, t, after):
        shrink = powers(t, -1)
        for q in (0, 2, 1, 3):
            for half in range(2):
                base = q * CH + half * 512
                part = jnp.dot(
                    ab[...], w_out[:, base : base + 512], preferred_element_type=F32
                )
                for g in range(4):
                    group = base // HD + g
                    scaled = part[:, g * HD : (g + 1) * HD] * shrink[:, group : group + 1]
                    pb[j, :, base + g * HD : base + (g + 1) * HD] = jnp.clip(
                        scaled, -127.0, 127.0
                    ).astype(BF16)
            after(q)

    def add_in(slot, others, q):
        def tile(i, c):
            rows = pl.ds(pl.multiple_of(i * 16, 16), 16)
            total = pb[slot, rows, cols(q)].astype(F32)
            for other in others:
                total = total + rb[other, rows, cols(q)].astype(F32)
            pb[slot, rows, cols(q)] = total.astype(BF16)
            return c

        lax.fori_loop(0, ROWS_B // 16, tile, 0)

    def when(j, k, action):
        pl.when(j == k)(action)

    def before(j):
        @functools.partial(when, j, 1)
        def _():
            arrived("own_up", (0, 1))
            send("far_up")
            arrived("own_down", (2, 3))
            send("far_down")
            arrived("own_up", (2, 3))

        @functools.partial(when, j, 2)
        def _():
            arrived("own_across")
            send("side_up")
            send("side_down")
            arrived("own_down", (0, 1))
            arrived("far_up", (0,))
            send("far_across", (0,))
            arrived("far_down", (2,))
            send("far_across", (2,))

        @functools.partial(when, j, 3)
        def _():
            arrived("far_up", (1,))
            send("far_across", (1,))
            arrived("far_down", (3,))
            send("far_across", (3,))
            send("r_near_down", (2, 3))
            send("r_near_up", (0, 1))

        @functools.partial(when, j, 5)
        def _():
            arrived("far_across")

        @functools.partial(when, j, 6)
        def _():
            arrived("side_up")

        @functools.partial(when, j, 7)
        def _():
            arrived("side_down")
            far_in((0, 2))

    def far_in(quarters):
        for q in quarters:
            arrived("r_far", (q,))
            add_in(4, (R_FAR,), q)
            send("r_half_down" if q < 2 else "r_half_up", (q,))

    def step(j, c):
        dx = (DX_BITS >> j) & 1
        dy = (DY_BITS >> (2 * j)) & 3
        t = ((mx + dx) % 2) * 4 + (my + dy) % 4
        before(j)
        norm(j)
        project()
        attend(t)

        def after(q):
            when(j, 5, lambda: send("r_far", (q,)))
            when(j, 6, lambda: send("r_side_down", (q,)))
            when(j, 7, lambda: send("r_side_up", (q,)))

        out_project(j, t, after)
        return c

    load_q.wait()
    load_k.wait()
    load_v.wait()
    load_kv.wait()
    load_o.wait()
    lax.fori_loop(0, 8, step, 0)

    far_in((1, 3))
    for q in (0, 2, 1, 3):
        arrived("r_side_down", (q,))
        arrived("r_side_up", (q,))
        add_in(3, (R_SIDE_P, R_SIDE_M), q)
        send("r_across", (q,))
        if q < 2:
            arrived("r_half_down", (q,))
            add_in(1, (R_HALF,), q)
            send("r_near_down", (q,))
        else:
            arrived("r_half_up", (q,))
            add_in(2, (R_HALF,), q)
            send("r_near_up", (q,))

    restore = powers(me, 1)
    outs = []
    for q in (0, 2, 1, 3):
        arrived("r_across", (q,))
        arrived("r_near_down", (q,))
        arrived("r_near_up", (q,))
        for g in range(CH // HD):
            group = q * (CH // HD) + g
            at = slice(group * HD, (group + 1) * HD)
            total = pb[0, :, at].astype(F32)
            for r in (R_P, R_M, R_X):
                total = total + rb[r, :, at].astype(F32)
            mixed = xg[0, :, at].astype(F32) + total * restore[:, group : group + 1]
            obuf[:, at] = mixed.astype(BF16)
        copy = pltpu.make_async_copy(obuf.at[:, cols(q)], out_hbm.at[:, cols(q)], out_sem.at[q])
        copy.start()
        outs.append(copy)
    for copy in outs:
        copy.wait()
    for name, spec in ROUTES.items():
        for q in spec[5]:
            route(name, q).wait_send()


def tables():
    position = (np.arange(ROWS_B) % NEW + CACHE).astype(np.float32)
    frequency = THETA ** (-(np.arange(HD // 2, dtype=np.float32) * np.float32(2.0)) / np.float32(HD))
    angles = position[:, None] * frequency.astype(np.float32)[None, :]
    cosine, sine = np.cos(angles), np.sin(angles)
    row = np.arange(ROWS_B)
    padded = row // NEW * 16 + row % NEW
    spread = np.zeros((PADDED, ROWS_B), np.float32)
    spread[padded, row] = 1.0
    return (
        jnp.asarray(np.concatenate([cosine, cosine], 1), F32),
        jnp.asarray(np.concatenate([-sine, sine], 1), F32),
        jnp.asarray(spread, BF16),
        jnp.asarray(spread.T, BF16),
    )


def on_device(
    tokens, norm_gain, query_weight, key_weight, value_weight, out_weight, past_cache, exponents
):
    seqs = past_cache.shape[0]
    pairs = past_cache.reshape(seqs, 2 * CACHE, HD)
    vmem = pl.BlockSpec(memory_space=pltpu.VMEM)
    anywhere = pl.BlockSpec(memory_space=pl.ANY)
    routes = len(ROUTES) * NQ
    return pl.pallas_call(
        body,
        out_shape=jax.ShapeDtypeStruct(tokens.shape, BF16),
        in_specs=[
            anywhere, vmem, anywhere, anywhere, anywhere, anywhere, anywhere, vmem, vmem, vmem,
            vmem, vmem,
        ],
        out_specs=anywhere,
        scratch_shapes=[
            pltpu.VMEM((8, ROWS_B, D), BF16),
            pltpu.VMEM((8, ROWS_B, D), BF16),
            pltpu.VMEM((7, ROWS_B, D), BF16),
            pltpu.VMEM((D, QC + 2 * HD), BF16),
            pltpu.VMEM((QC, D), BF16),
            pltpu.VMEM((seqs, 2 * CACHE, HD), BF16),
            pltpu.VMEM((ROWS_B, D), BF16),
            pltpu.VMEM((PADDED, QC + 2 * HD), BF16),
            pltpu.VMEM((PADDED, QC), BF16),
            pltpu.VMEM((ROWS_B, QC), BF16),
            pltpu.VMEM((ROWS_B, D), BF16),
            pltpu.SemaphoreType.DMA((9,)),
            pltpu.SemaphoreType.DMA((routes,)),
            pltpu.SemaphoreType.DMA((routes,)),
            pltpu.SemaphoreType.DMA((NQ,)),
        ],
        compiler_params=pltpu.CompilerParams(
            collective_id=0, has_side_effects=True, vmem_limit_bytes=67_000_000
        ),
        name="verify_block",
    )(
        tokens, norm_gain.reshape(1, D), query_weight, key_weight, value_weight, out_weight, pairs,
        exponents, *tables(),
    )


def solution(mesh):
    return jax.shard_map(
        on_device,
        mesh=mesh,
        in_specs=(
            P(("dp", "tensor"), None),
            P(),
            P(None, "tensor"),
            P(None, "tensor"),
            P(None, "tensor"),
            P("tensor", None),
            P("dp", None, None, "tensor"),
            P("dp", None),
        ),
        out_specs=P(("dp", "tensor"), None),
        check_vma=False,
    )
```

time: 443 us -> 198 us (0.45); the launches traced: 435 us -> 198 us
  waiting for transfers between devices: 204 us -> 0 us
  Pallas kernels: 0 us -> 192 us
  local copies, waits for them, and re-layouts: 104 us -> 5.78 us
  matrix products: 71.4 us -> 0 us
  other arithmetic: 41 us -> 0 us
  between operations: 13.7 us -> 0.01 us
    pallas_call x0 -> x1, Pallas kernels: none -> 192 us  [on_device(): pl.pallas_call(body, out_shape=jax.ShapeDtypeStruct(tokens.shape, BF16),...]
    reduce_scatter x1 -> x0, waiting for transfers between devices: 110 us -> none  [on_device(): lax.psum_scatter(rounded.astype(jnp.bfloat16), 'tensor', scatter_dimensio...]
    all_gather x2 -> x0, waiting for transfers between devices: 93.2 us -> none  [work_in_pieces(): finished.append(jax.vmap(apply)(lax.all_gather(share, axis), starts))]
    dot_general x11 -> x0, matrix products: 71.4 us -> none  [the longest x1 16.1 us: on_device(): jnp.dot(attended, out_weight, preferred_element_type=jnp.float32)]
    slice x5 -> x0, local copies, waits for them, and re-layouts: 22.6 us -> none  [the longest x1 15.5 us: attention(): past_cache[:, :, 1].reshape(seq_count, cache_len, kv_heads, HD)]
    reduce_sum x4 -> x0, other arithmetic: 18.6 us -> none  [the longest x2 11.3 us: attention(): denominator = (cache_probs.sum(-1) + new_probs.sum(-1))[..., None]]
    convert_element_type x4 -> x0, local copies, waits for them, and re-layouts: 17.8 us -> none  [the longest x1 9.33 us: on_device(): query = rotate(projected[:, :query_cols], query_local).astype(jnp.bfloat16)]
    unnamed x31 -> x2, local copies, waits for them, and re-layouts: 21.8 us -> 4.48 us
  transfers between devices with their start and end apart: 3 -> 0, of which waited for: 3 -> 0; matrix products, arithmetic and copies ran while one was open for 8% -> 0% of each run, Pallas kernels for 0% -> 0%
where the time goes in v1:
time: 198 us
  Pallas kernels  192 us (97%)
  local copies, waits for them, and re-layouts  5.78 us (3%)
    pallas_call x1, Pallas kernels, on_device(): pl.pallas_call(body, out_shape=jax.ShapeDtypeStruct(tokens.shape, BF16),...  192 us
    unnamed x2, local copies, waits for them, and re-layouts  4.48 us

profile of v1, /device:TPU:0, one launch (start us, length us, event | category | flops | bytes accessed | tf_op | source)
XLA Modules:
  0.0 197.6 jit_solution(12540108318590684497)
XLA Ops:
  0.0 1.3 reshape.6.gain_ref
  1.3 2.0 %copy.13.exps_ref = s32[1280,32]{1,0:T(8,128)} copy(s32[1280,32]{0,1:T(8,128)} %param.19) | data formatting | bytes 327680 | tf_op args[7]
  3.3 191.8 %verify_block.1 = bf16[160,4096]{1,0:T(8,128)(2,1)} custom-call(bf16[160,4096]{1,0:T(8,128)(2,1)} %tokens_hbm.1, bf16[1,4096]{1,0:T(2,128)(2,1)} %reshape.6.gain_ref, bf16[4096,1024]{1,0:T(8,128)(2,1)} %wq_hbm.1, bf16[4096,128]{1,0:T(8,128)(2,1)} %wk_hbm.1, bf16[4096,128]{1,0:T(8,128)(2,1)} %wv_hbm.1, bf16[1024,4096]{1,0:T(8,128)(2,1)} %wo_hbm.1, ...), custom_call_target="tpu_custom_call" | custom-call | tf_op jit(solution)/shard_map/verify_block/pallas_call | solution.py:358
  195.1 2.5 %copy.15 = bf16[160,4096]{1,0:T(8,128)(2,1)} copy(bf16[160,4096]{1,0:T(8,128)(2,1)} %verify_block.1) | data formatting | bytes 2621440

commit v2 on v1

v2 whole, which is shorter than its diff:
```python
import functools

import jax
import jax.numpy as jnp
import numpy as np
from jax import lax
from jax.experimental import pallas as pl
from jax.experimental.pallas import tpu as pltpu
from jax.sharding import PartitionSpec as P

HD = 128
NEW = 10
CACHE = 64
D = 4096
HEADS = 8
QC = 1024
SEQ_BLOCK = 16
ROWS_B = 160
PADDED = 256
SPREAD = 512
CH = 1024
NQ = 4
EPS = 1e-05
THETA = 500000.0
MESH = pl.DeviceIdType.MESH
F32 = jnp.float32
BF16 = jnp.bfloat16
SCORE = float(np.log2(np.e) / np.sqrt(HD))

SLOTS = ((0, 0), (0, 3), (0, 1), (1, 0), (0, 2), (1, 2), (1, 3), (1, 1))
DX_BITS = sum(dx << j for j, (dx, _) in enumerate(SLOTS))
DY_BITS = sum(dy << (2 * j) for j, (_, dy) in enumerate(SLOTS))

UP, DOWN, ACROSS, BEYOND, ZUP, ZDOWN, CORE = range(7)
OWN, NEAR_M, NEAR_P, FAR = range(4)
R_HALF, R_P, R_M = range(3)

QUARTERS = [(q * CH, CH) for q in range(NQ)]
SIDE = [(0, 1024), (1024, 1024), (2048, 1024), (3072, 512)]
REST = [(3584, 512)]
ROUTES = {
    "own_up": (UP, "x", 0, "x", 1, QUARTERS),
    "own_down": (DOWN, "x", 0, "x", 2, QUARTERS),
    "own_across": (ACROSS, "x", 0, "x", 3, QUARTERS),
    "far_up": (UP, "x", 1, "x", 4, QUARTERS[:2]),
    "far_down": (DOWN, "x", 2, "x", 4, QUARTERS[2:]),
    "far_across": (ACROSS, "x", 4, "x", 5, QUARTERS),
    "side_up": (UP, "x", 3, "x", 6, SIDE),
    "side_down": (DOWN, "x", 3, "x", 7, SIDE),
    "rest_m": (ACROSS, "x", 1, "x", 6, REST),
    "rest_p": (ACROSS, "x", 2, "x", 7, REST),
    "att_own": (ACROSS, "a", 3, "b", OWN, [(0, QC)]),
    "att_far": (ACROSS, "a", 5, "b", FAR, [(0, QC)]),
    "att_near_m": (ACROSS, "a", 6, "b", NEAR_M, [(0, QC)]),
    "att_near_p": (ACROSS, "a", 7, "b", NEAR_P, [(0, QC)]),
    "half_down": (DOWN, "p", FAR, "r", R_HALF, QUARTERS[:2]),
    "half_up": (UP, "p", FAR, "r", R_HALF, QUARTERS[2:]),
    "sum_down": (DOWN, "p", NEAR_M, "r", R_P, QUARTERS),
    "sum_up": (UP, "p", NEAR_P, "r", R_M, QUARTERS),
}
WEIGHTS = {
    "w_beyond": (BEYOND, True, 0, (0, 1, 2, 3)),
    "w_zup": (ZUP, False, 0, (0, 1, 2, 3)),
    "w_zdown": (ZDOWN, False, 0, (0, 1, 2, 3)),
    "w_fwd_up": (ZUP, False, 3, (0, 1)),
    "w_fwd_down": (ZDOWN, False, 1, (2, 3)),
    "w_core0": (CORE, False, 0, (None,)),
    "w_core3": (CORE, False, 3, (None,)),
    "w_core1": (CORE, False, 1, (None,)),
    "w_core2": (CORE, False, 2, (None,)),
}
BASE = {}
COUNT = 0
for _name, _spec in ROUTES.items():
    BASE[_name] = COUNT
    COUNT += len(_spec[5])
for _name, _spec in WEIGHTS.items():
    BASE[_name] = COUNT
    COUNT += len(_spec[3])
PIECE = QC // 8
SUB = PIECE // 4


def body(
    tokens_hbm, gain_ref, wq_hbm, wk_hbm, wv_hbm, wo_hbm, kv_hbm, exps_ref, cos_ref, sin_ref,
    pad_ref, unpad_ref, pad_k_ref, pad_v_ref, parity_ref, out_hbm,
    xg, pb, rb, ab, bb, w_in, w_out, w_two, kv, xn, qkv, qp, kp, vp, ap, obuf, exps, gains,
    load_sem, send_sem, recv_sem, out_sem,
):
    me = lax.axis_index("tensor")
    mx, my = me // 4, me % 4
    dp = lax.axis_index("dp")
    hi, z, core = dp // 8, (dp // 2) % 4, dp % 2
    other = (1 - mx) * 4 + my
    z_next, z_last = (z + 1) % 4, (z + 3) % 4
    targets = {
        UP: {"tensor": mx * 4 + (my + 1) % 4},
        DOWN: {"tensor": mx * 4 + (my + 3) % 4},
        ACROSS: {"tensor": other},
        BEYOND: {"dp": (1 - hi) * 8 + z * 2 + core, "tensor": other},
        ZUP: {"dp": hi * 8 + z_next * 2 + core},
        ZDOWN: {"dp": hi * 8 + z_last * 2 + core},
        CORE: {"dp": hi * 8 + z * 2 + (1 - core)},
    }
    buffers = {"x": xg, "p": pb, "r": rb, "a": ab, "b": bb}

    def route(name, i):
        k = BASE[name] + i
        if name in ROUTES:
            target, sbuf, sslot, dbuf, dslot, pieces = ROUTES[name]
            at = pl.ds(*pieces[i])
            src, dst = buffers[sbuf].at[sslot, :, at], buffers[dbuf].at[dslot, :, at]
        else:
            target, mine, dz, subs = WEIGHTS[name]
            first = (((z + dz) % 4) * 2 + core) * PIECE
            if subs[i] is None:
                rows = pl.ds(pl.multiple_of(first, PIECE), PIECE)
            else:
                rows = pl.ds(pl.multiple_of(first + subs[i] * SUB, SUB), SUB)
            src, dst = (w_out if mine else w_two).at[rows, :], w_two.at[rows, :]
        return pltpu.make_async_remote_copy(
            src_ref=src, dst_ref=dst, send_sem=send_sem.at[k], recv_sem=recv_sem.at[k],
            device_id=targets[target], device_id_type=MESH,
        )

    def pieces_of(name, which):
        if which is not None:
            return which
        return range(len(ROUTES[name][5] if name in ROUTES else WEIGHTS[name][3]))

    def send(name, which=None):
        for i in pieces_of(name, which):
            route(name, i).start()

    def arrived(name, which=None):
        for i in pieces_of(name, which):
            received(name, i).wait_recv()

    def received(name, i):
        if name in ROUTES:
            return route(name, i)
        k = BASE[name] + i
        target, _, dz, subs = WEIGHTS[name]
        sender_z = {BEYOND: z, ZUP: z_last, ZDOWN: z_next, CORE: z}[target]
        sender_core = (1 - core) if target == CORE else core
        first = (((sender_z + dz) % 4) * 2 + sender_core) * PIECE
        if subs[i] is None:
            rows = pl.ds(pl.multiple_of(first, PIECE), PIECE)
        else:
            rows = pl.ds(pl.multiple_of(first + subs[i] * SUB, SUB), SUB)
        return pltpu.make_async_remote_copy(
            src_ref=w_two.at[rows, :], dst_ref=w_two.at[rows, :], send_sem=send_sem.at[k],
            recv_sem=recv_sem.at[k], device_id=targets[target], device_id_type=MESH,
        )

    load_x = pltpu.make_async_copy(tokens_hbm, xg.at[0], load_sem.at[0])
    load_o = pltpu.make_async_copy(wo_hbm, w_out, load_sem.at[1])
    load_q = pltpu.make_async_copy(wq_hbm, w_in.at[:, pl.ds(0, QC)], load_sem.at[2])
    load_k = pltpu.make_async_copy(wk_hbm, w_in.at[:, pl.ds(QC, HD)], load_sem.at[3])
    load_v = pltpu.make_async_copy(wv_hbm, w_in.at[:, pl.ds(QC + HD, HD)], load_sem.at[4])
    load_kv = pltpu.make_async_copy(kv_hbm, kv, load_sem.at[5])
    for copy in (load_x, load_o, load_q, load_k, load_v, load_kv):
        copy.start()

    barrier = pltpu.get_barrier_semaphore()
    for target in targets.values():
        pl.semaphore_signal(barrier, inc=1, device_id=target, device_id_type=MESH)
    pl.semaphore_wait(barrier, len(targets))

    load_x.wait()
    for i in range(NQ):
        send("own_up", (i,))
        send("own_down", ((i + 2) % NQ,))
        send("own_across", (i,))
    load_o.wait()
    send("w_beyond")

    gain = gain_ref[...].astype(F32)
    for g in range(D // HD):
        gains[:, g * HD : (g + 1) * HD] = jnp.broadcast_to(gain[g : g + 1], (16, HD))
    fill = jnp.zeros((HD - 32, HD), F32)
    for i in range(8 * ROWS_B // HD):
        at = slice(i * HD, (i + 1) * HD)
        exps[at, :] = jnp.concatenate([exps_ref[:, at].astype(F32), fill], 0).T

    def norm(j):
        def some(i5, c):
            scales = []
            for i in range(5):
                rows = pl.ds(pl.multiple_of((i5 * 5 + i) * 16, 16), 16)
                squares = None
                for g in range(D // HD):
                    x = xg[j, rows, g * HD : (g + 1) * HD].astype(F32)
                    squares = x * x if g == 0 else squares + x * x
                scales.append(squares)
            scales = [lax.rsqrt(jnp.sum(s, axis=-1, keepdims=True) * (1.0 / D) + EPS) for s in scales]
            for i in range(5):
                rows = pl.ds(pl.multiple_of((i5 * 5 + i) * 16, 16), 16)
                xn[rows, :] = (xg[j, rows, :].astype(F32) * scales[i] * gains[...]).astype(BF16)
            return c

        lax.fori_loop(0, 2, some, 0)

    def rot(m):
        return m * cos_ref[...] + pltpu.roll(m, HD // 2, 1) * sin_ref[...]

    def project():
        for n in range(5):
            at = slice(n * 256, (n + 1) * 256)
            m = jnp.dot(xn[...], w_in[:, at], preferred_element_type=F32)
            second = rot(m[:, HD:]) if n < 4 else m[:, HD:]
            qkv[:, at] = jnp.concatenate([rot(m[:, :HD]), second], 1).astype(BF16)
        for n in range(4):
            at = slice(n * 256, (n + 1) * 256)
            qp[:, at] = jnp.dot(pad_ref[...], qkv[:, at], preferred_element_type=F32).astype(BF16)
        kp[...] = jnp.dot(
            pad_k_ref[...], qkv[:, QC : QC + HD], preferred_element_type=F32
        ).astype(BF16)
        vp[...] = jnp.dot(pad_v_ref[...], qkv[:, QC + HD :], preferred_element_type=F32).astype(BF16)

    def attend(j, t):
        lane = lax.broadcasted_iota(jnp.int32, (HD, HD), 1)
        token = lax.broadcasted_iota(jnp.int32, (HD, HD), 0) % 16
        seen = (lane % 2 == 0) | (lane <= 2 * token + 1)
        contract_last = (((1,), (1,)), ((), ()))
        batch = 4

        def some(s4, c):
            scores, values = [], []
            for i in range(batch):
                s = s4 * batch + i
                rows = pl.ds(pl.multiple_of(s * 16, 16), 16)
                spread = pl.ds(pl.multiple_of(s * 32, 32), 32)
                query = jnp.concatenate([qp[rows, h * HD : (h + 1) * HD] for h in range(HEADS)], 0)
                pairs = kv[t * SEQ_BLOCK + s]
                keys = jnp.concatenate([pairs[:32] * parity_ref[0] + kp[spread, :], pairs[32:]], 0)
                values.append(
                    jnp.concatenate([pairs[:32] * parity_ref[1] + vp[spread, :], pairs[32:]], 0)
                )
                scores.append(
                    lax.dot_general(query, keys, contract_last, preferred_element_type=F32)
                )
            scores = [jnp.where(seen, x, -1e30) for x in scores]
            tops = [jnp.max(x, axis=1, keepdims=True) for x in scores]
            raised = [jnp.exp2((x - top) * SCORE) for x, top in zip(scores, tops)]
            totals = [jnp.sum(x, axis=1, keepdims=True) for x in raised]
            probs = [(x * (1.0 / total)).astype(BF16) for x, total in zip(raised, totals)]
            for i in range(batch):
                rows = pl.ds(pl.multiple_of((s4 * batch + i) * 16, 16), 16)
                p = pltpu.roll(probs[i], 1, 1)
                att = jnp.dot(p, values[i], preferred_element_type=F32).astype(BF16)
                for h in range(HEADS):
                    ap[rows, h * HD : (h + 1) * HD] = att[h * 16 : (h + 1) * 16]
            return c

        lax.fori_loop(0, SEQ_BLOCK // batch, some, 0)
        for n in range(4):
            at = slice(n * 256, (n + 1) * 256)
            ab[j, :, at] = jnp.dot(
                unpad_ref[...], ap[:, at], preferred_element_type=F32
            ).astype(BF16)

    def powers(t, sign):
        e = exps[pl.ds(pl.multiple_of(t * ROWS_B, ROWS_B), ROWS_B), :].astype(jnp.int32)
        if sign < 0:
            return jnp.left_shift(1, -e).astype(F32)
        return jnp.left_shift(1, e + 11).astype(F32) * (2.0**-11)

    def out_project(att, weights, k, t, order, extra, done):
        shrink = powers(t, -1)
        for q in order:
            for base in (q * CH, q * CH + 512):
                part = jnp.dot(att, weights[:, base : base + 512], preferred_element_type=F32)
                for g in range(4):
                    at = slice(base + g * HD, base + (g + 1) * HD)
                    group = base // HD + g
                    scaled = part[:, g * HD : (g + 1) * HD] * shrink[:, group : group + 1]
                    scaled = jnp.clip(scaled, -127.0, 127.0).astype(BF16)
                    for r in extra(q, g == 0 and base == q * CH):
                        scaled = scaled.astype(F32) + r[:, at].astype(F32)
                    pb[k, :, at] = scaled.astype(BF16)
            done(q)

    def column_block(j):
        return j - (j // 4)

    def second(k, dy, order, half, name):
        t = mx * 4 + (my + dy) % 4

        def extra(q, first):
            refs = [pb.at[k]]
            if half is not None and q in half[1]:
                if first:
                    arrived(half[0], (half[1].index(q),))
                refs.append(rb.at[R_HALF])
            return refs

        def done(q):
            if name == "half":
                send("half_down" if q < 2 else "half_up", (q % 2,))
            elif name:
                send(name, (q,))

        out_project(bb[k], w_two, k, t, order, extra, done)

    def when(j, k, action):
        pl.when(j == k)(action)

    def before(j):
        @functools.partial(when, j, 1)
        def _():
            arrived("own_up", (0,))
            send("far_up", (0,))
            arrived("own_down", (2,))
            send("far_down", (0,))
            for i in range(4):
                arrived("w_beyond", (i,))
                send("w_zup", (i,))
                send("w_zdown", (i,))
                if i == 1:
                    arrived("own_up", (1,))
                    send("far_up", (1,))
                    arrived("own_down", (3,))
                    send("far_down", (1,))
            send("w_core0")
            arrived("own_up", (2, 3))
            send("rest_m")
            arrived("own_down", (0, 1))
            send("rest_p")
            arrived("own_across")
            send("side_up")
            send("side_down")

        @functools.partial(when, j, 2)
        def _():
            arrived("far_up", (0,))
            send("far_across", (0,))
            arrived("far_down", (0,))
            send("far_across", (2,))
            arrived("w_zup", (0, 1))
            send("w_fwd_up")
            arrived("w_zdown", (2, 3))
            send("w_fwd_down")

        @functools.partial(when, j, 3)
        def _():
            arrived("far_up", (1,))
            send("far_across", (1,))
            arrived("far_down", (1,))
            send("far_across", (3,))

        @functools.partial(when, j, 4)
        def _():
            send("att_own")
            arrived("w_zup", (2, 3))
            send("w_core3")
            arrived("w_zdown", (0, 1))
            send("w_core1")

        @functools.partial(when, j, 5)
        def _():
            arrived("w_fwd_up")
            arrived("w_fwd_down")
            send("w_core2")
            arrived("far_across")

        @functools.partial(when, j, 6)
        def _():
            send("att_far")
            arrived("rest_m")
            arrived("side_up")

        @functools.partial(when, j, 7)
        def _():
            send("att_near_m")
            for name in ("w_core0", "w_core3", "w_core1", "w_core2"):
                arrived(name)
            arrived("att_far")
            second(FAR, 2, (0, 2, 1, 3), None, "half")
            arrived("rest_p")
            arrived("side_down")

    def step(j, c):
        dx = (DX_BITS >> j) & 1
        dy = (DY_BITS >> (2 * j)) & 3
        t = ((mx + dx) % 2) * 4 + (my + dy) % 4
        before(j)
        norm(j)
        project()
        attend(j, t)

        @pl.when(dx == 0)
        def _():
            out_project(
                ab[j], w_out, column_block(j), t, range(NQ), lambda q, first: (), lambda q: None
            )

        return c

    load_q.wait()
    load_k.wait()
    load_v.wait()
    load_kv.wait()
    lax.fori_loop(0, 8, step, 0)

    send("att_near_p")
    arrived("att_near_m")
    second(NEAR_M, 3, (2, 3, 0, 1), ("half_down", (0, 1)), "sum_down")
    arrived("att_own")
    second(OWN, 0, range(NQ), None, None)
    arrived("att_near_p")
    second(NEAR_P, 1, (0, 1, 2, 3), ("half_up", (2, 3)), "sum_up")

    restore = powers(me, 1)
    outs = []
    for q in range(NQ):
        arrived("sum_down", (q,))
        arrived("sum_up", (q,))
        for g in range(CH // HD):
            group = q * (CH // HD) + g
            at = slice(group * HD, (group + 1) * HD)
            total = pb[OWN, :, at].astype(F32)
            for r in (R_P, R_M):
                total = total + rb[r, :, at].astype(F32)
            mixed = xg[0, :, at].astype(F32) + total * restore[:, group : group + 1]
            obuf[:, at] = mixed.astype(BF16)
        at = pl.ds(*QUARTERS[q])
        copy = pltpu.make_async_copy(obuf.at[:, at], out_hbm.at[:, at], out_sem.at[q])
        copy.start()
        outs.append(copy)
    for copy in outs:
        copy.wait()
    for name in (*ROUTES, *WEIGHTS):
        for i in pieces_of(name, None):
            route(name, i).wait_send()


def tables():
    position = (np.arange(ROWS_B) % NEW + CACHE).astype(np.float32)
    frequency = THETA ** (-(np.arange(HD // 2, dtype=np.float32) * np.float32(2.0)) / np.float32(HD))
    angles = position[:, None] * frequency.astype(np.float32)[None, :]
    cosine, sine = np.cos(angles), np.sin(angles)
    row = np.arange(ROWS_B)
    spread = np.zeros((PADDED, ROWS_B), np.float32)
    spread[row // NEW * 16 + row % NEW, row] = 1.0
    keys = np.zeros((SPREAD, ROWS_B), np.float32)
    keys[row // NEW * 32 + 2 * (row % NEW) + 1, row] = 1.0
    values = np.zeros((SPREAD, ROWS_B), np.float32)
    values[row // NEW * 32 + 2 * (row % NEW) + 2, row] = 1.0
    even = np.broadcast_to((np.arange(32) % 2 == 0)[:, None], (32, HD))
    return (
        jnp.asarray(np.concatenate([cosine, cosine], 1), F32),
        jnp.asarray(np.concatenate([-sine, sine], 1), F32),
        jnp.asarray(spread, BF16),
        jnp.asarray(spread.T, BF16),
        jnp.asarray(keys, BF16),
        jnp.asarray(values, BF16),
        jnp.asarray(np.stack([even, ~even]), BF16),
    )


def on_device(
    tokens, norm_gain, query_weight, key_weight, value_weight, out_weight, past_cache, exponents
):
    seqs = past_cache.shape[0]
    pairs = past_cache.reshape(seqs, 2 * CACHE, HD)
    vmem = pl.BlockSpec(memory_space=pltpu.VMEM)
    anywhere = pl.BlockSpec(memory_space=pl.ANY)
    return pl.pallas_call(
        body,
        out_shape=jax.ShapeDtypeStruct(tokens.shape, BF16),
        in_specs=[anywhere, vmem, *[anywhere] * 5, *[vmem] * 8],
        out_specs=anywhere,
        scratch_shapes=[
            pltpu.VMEM((8, ROWS_B, D), BF16),
            pltpu.VMEM((4, ROWS_B, D), BF16),
            pltpu.VMEM((3, ROWS_B, D), BF16),
            pltpu.VMEM((8, ROWS_B, QC), BF16),
            pltpu.VMEM((4, ROWS_B, QC), BF16),
            pltpu.VMEM((D, QC + 2 * HD), BF16),
            pltpu.VMEM((QC, D), BF16),
            pltpu.VMEM((QC, D), BF16),
            pltpu.VMEM((seqs, 2 * CACHE, HD), BF16),
            pltpu.VMEM((ROWS_B, D), BF16),
            pltpu.VMEM((ROWS_B, QC + 2 * HD), BF16),
            pltpu.VMEM((PADDED, QC), BF16),
            pltpu.VMEM((SPREAD, HD), BF16),
            pltpu.VMEM((SPREAD, HD), BF16),
            pltpu.VMEM((PADDED, QC), BF16),
            pltpu.VMEM((ROWS_B, D), BF16),
            pltpu.VMEM((8 * ROWS_B, HD), F32),
            pltpu.VMEM((16, D), F32),
            pltpu.SemaphoreType.DMA((6,)),
            pltpu.SemaphoreType.DMA((COUNT,)),
            pltpu.SemaphoreType.DMA((COUNT,)),
            pltpu.SemaphoreType.DMA((NQ,)),
        ],
        compiler_params=pltpu.CompilerParams(
            collective_id=0, has_side_effects=True, vmem_limit_bytes=67_000_000
        ),
        name="verify_block",
    )(
        tokens, norm_gain.reshape(D // HD, HD), query_weight, key_weight, value_weight, out_weight,
        pairs, exponents.T, *tables(),
    )


def solution(mesh):
    return jax.shard_map(
        on_device,
        mesh=mesh,
        in_specs=(
            P(("dp", "tensor"), None),
            P(),
            P(None, "tensor"),
            P(None, "tensor"),
            P(None, "tensor"),
            P("tensor", None),
            P("dp", None, None, "tensor"),
            P("dp", None),
        ),
        out_specs=P(("dp", "tensor"), None),
        check_vma=False,
    )
```

time: 198 us -> 135 us (0.68)
  Pallas kernels: 192 us -> 132 us
  local copies, waits for them, and re-layouts: 5.78 us -> 2.49 us
    pallas_call x1, Pallas kernels: 192 us -> 132 us  [on_device(): pl.pallas_call(body, out_shape=jax.ShapeDtypeStruct(tokens.shape, BF16),...]
    unnamed x2 -> x1, local copies, waits for them, and re-layouts: 4.48 us -> 2.49 us
where the time goes in v2:
time: 135 us
  Pallas kernels  132 us (98%)
  local copies, waits for them, and re-layouts  2.49 us (2%)
    pallas_call x1, Pallas kernels, on_device(): pl.pallas_call(body, out_shape=jax.ShapeDtypeStruct(tokens.shape, BF16),...  132 us

profile of v2, /device:TPU:0, one launch (start us, length us, event | category | flops | bytes accessed | tf_op | source)
XLA Modules:
  0.0 134.7 jit_solution(15132632917022296960)
XLA Ops:
  0.0 132.2 %verify_block.1 = bf16[160,4096]{1,0:T(8,128)(2,1)} custom-call(bf16[160,4096]{1,0:T(8,128)(2,1)} %tokens_hbm.1, bf16[32,128]{1,0:T(8,128)(2,1)} %bitcast.5, bf16[4096,1024]{1,0:T(8,128)(2,1)} %wq_hbm.1, bf16[4096,128]{1,0:T(8,128)(2,1)} %wk_hbm.1, bf16[4096,128]{1,0:T(8,128)(2,1)} %wv_hbm.1, bf16[1024,4096]{1,0:T(8,128)(2,1)} %wo_hbm.1, ...), custom_call_target="tpu_custom_call" | custom-call | tf_op jit(solution)/shard_map/verify_block/pallas_call | solution.py:469
  132.2 2.5 %copy.17 = bf16[160,4096]{1,0:T(8,128)(2,1)} copy(bf16[160,4096]{1,0:T(8,128)(2,1)} %verify_block.1) | data formatting | bytes 2621440

commit v3 on v2

--- a/solution.py
+++ b/solution.py
@@ -27,32 +27,33 @@
 BF16 = jnp.bfloat16
 SCORE = float(np.log2(np.e) / np.sqrt(HD))
 
-SLOTS = ((0, 0), (0, 3), (0, 1), (1, 0), (0, 2), (1, 2), (1, 3), (1, 1))
+SLOTS = ((0, 0), (1, 0), (0, 2), (0, 3), (0, 1), (1, 2), (1, 3), (1, 1))
 DX_BITS = sum(dx << j for j, (dx, _) in enumerate(SLOTS))
 DY_BITS = sum(dy << (2 * j) for j, (_, dy) in enumerate(SLOTS))
 
 UP, DOWN, ACROSS, BEYOND, ZUP, ZDOWN, CORE = range(7)
-OWN, NEAR_M, NEAR_P, FAR = range(4)
+OWN, FAR, NEAR_M, NEAR_P = range(4)
 R_HALF, R_P, R_M = range(3)
 
 QUARTERS = [(q * CH, CH) for q in range(NQ)]
 SIDE = [(0, 1024), (1024, 1024), (2048, 1024), (3072, 512)]
 REST = [(3584, 512)]
+HALVES = [(0, 80), (80, 80)]
 ROUTES = {
-    "own_up": (UP, "x", 0, "x", 1, QUARTERS),
-    "own_down": (DOWN, "x", 0, "x", 2, QUARTERS),
-    "own_across": (ACROSS, "x", 0, "x", 3, QUARTERS),
-    "far_up": (UP, "x", 1, "x", 4, QUARTERS[:2]),
-    "far_down": (DOWN, "x", 2, "x", 4, QUARTERS[2:]),
-    "far_across": (ACROSS, "x", 4, "x", 5, QUARTERS),
-    "side_up": (UP, "x", 3, "x", 6, SIDE),
-    "side_down": (DOWN, "x", 3, "x", 7, SIDE),
-    "rest_m": (ACROSS, "x", 1, "x", 6, REST),
-    "rest_p": (ACROSS, "x", 2, "x", 7, REST),
-    "att_own": (ACROSS, "a", 3, "b", OWN, [(0, QC)]),
-    "att_far": (ACROSS, "a", 5, "b", FAR, [(0, QC)]),
-    "att_near_m": (ACROSS, "a", 6, "b", NEAR_M, [(0, QC)]),
-    "att_near_p": (ACROSS, "a", 7, "b", NEAR_P, [(0, QC)]),
+    "own_up": (UP, "x", 0, "x", 3, QUARTERS),
+    "own_down": (DOWN, "x", 0, "x", 4, QUARTERS),
+    "own_across": (ACROSS, "x", 0, "x", 1, QUARTERS),
+    "far_up": (UP, "x", 3, "x", 2, QUARTERS[:2]),
+    "far_down": (DOWN, "x", 4, "x", 2, QUARTERS[2:]),
+    "far_across": (ACROSS, "x", 2, "x", 5, QUARTERS),
+    "side_up": (UP, "x", 1, "x", 6, SIDE),
+    "side_down": (DOWN, "x", 1, "x", 7, SIDE),
+    "rest_m": (ACROSS, "x", 3, "x", 6, REST),
+    "rest_p": (ACROSS, "x", 4, "x", 7, REST),
+    "att_own": (ACROSS, "a", 1, "b", OWN, HALVES),
+    "att_far": (ACROSS, "a", 5, "b", FAR, HALVES),
+    "att_near_m": (ACROSS, "a", 6, "b", NEAR_M, HALVES),
+    "att_near_p": (ACROSS, "a", 7, "b", NEAR_P, HALVES),
     "half_down": (DOWN, "p", FAR, "r", R_HALF, QUARTERS[:2]),
     "half_up": (UP, "p", FAR, "r", R_HALF, QUARTERS[2:]),
     "sum_down": (DOWN, "p", NEAR_M, "r", R_P, QUARTERS),
@@ -84,9 +85,10 @@
 def body(
     tokens_hbm, gain_ref, wq_hbm, wk_hbm, wv_hbm, wo_hbm, kv_hbm, exps_ref, cos_ref, sin_ref,
     pad_ref, unpad_ref, pad_k_ref, pad_v_ref, parity_ref, out_hbm,
-    xg, pb, rb, ab, bb, w_in, w_out, w_two, kv, xn, qkv, qp, kp, vp, ap, obuf, exps, gains,
+    xg, pb, rb, ab, bb, w_in, w_out, w_two, kv, xn, qkv, qp, kp, vp, ap, exps, gains,
     load_sem, send_sem, recv_sem, out_sem,
 ):
+    obuf = xn
     me = lax.axis_index("tensor")
     mx, my = me // 4, me % 4
     dp = lax.axis_index("dp")
@@ -109,7 +111,10 @@
         if name in ROUTES:
             target, sbuf, sslot, dbuf, dslot, pieces = ROUTES[name]
             at = pl.ds(*pieces[i])
-            src, dst = buffers[sbuf].at[sslot, :, at], buffers[dbuf].at[dslot, :, at]
+            if sbuf == "a":
+                src, dst = ab.at[sslot, at, :], bb.at[dslot, at, :]
+            else:
+                src, dst = buffers[sbuf].at[sslot, :, at], buffers[dbuf].at[dslot, :, at]
         else:
             target, mine, dz, subs = WEIGHTS[name]
             first = (((z + dz) % 4) * 2 + core) * PIECE
@@ -169,8 +174,9 @@
 
     load_x.wait()
     for i in range(NQ):
-        send("own_up", (i,))
-        send("own_down", ((i + 2) % NQ,))
+        if i < 2:
+            send("own_up", (i,))
+            send("own_down", (i + 2,))
         send("own_across", (i,))
     load_o.wait()
     send("w_beyond")
@@ -218,7 +224,7 @@
         ).astype(BF16)
         vp[...] = jnp.dot(pad_v_ref[...], qkv[:, QC + HD :], preferred_element_type=F32).astype(BF16)
 
-    def attend(j, t):
+    def attend(j, t, half):
         lane = lax.broadcasted_iota(jnp.int32, (HD, HD), 1)
         token = lax.broadcasted_iota(jnp.int32, (HD, HD), 0) % 16
         seen = (lane % 2 == 0) | (lane <= 2 * token + 1)
@@ -253,11 +259,14 @@
                     ap[rows, h * HD : (h + 1) * HD] = att[h * 16 : (h + 1) * 16]
             return c
 
-        lax.fori_loop(0, SEQ_BLOCK // batch, some, 0)
+        parts = SEQ_BLOCK // batch // 2
+        lax.fori_loop(half * parts, (half + 1) * parts, some, 0)
+        rows = slice(half * 80, (half + 1) * 80)
         for n in range(4):
             at = slice(n * 256, (n + 1) * 256)
-            ab[j, :, at] = jnp.dot(
-                unpad_ref[...], ap[:, at], preferred_element_type=F32
+            padded = ap[half * 128 : (half + 1) * 128, at]
+            ab[j, rows, at] = jnp.dot(
+                unpad_ref[...], padded, preferred_element_type=F32
             ).astype(BF16)
 
     def powers(t, sign):
@@ -282,7 +291,7 @@
             done(q)
 
     def column_block(j):
-        return j - (j // 4)
+        return j - (j + 7) // 8
 
     def second(k, dy, order, half, name):
         t = mx * 4 + (my + dy) % 4
@@ -311,8 +320,10 @@
         def _():
             arrived("own_up", (0,))
             send("far_up", (0,))
+            send("own_up", (2,))
             arrived("own_down", (2,))
             send("far_down", (0,))
+            send("own_down", (0,))
             for i in range(4):
                 arrived("w_beyond", (i,))
                 send("w_zup", (i,))
@@ -320,38 +331,36 @@
                 if i == 1:
                     arrived("own_up", (1,))
                     send("far_up", (1,))
+                    send("own_up", (3,))
                     arrived("own_down", (3,))
                     send("far_down", (1,))
+                    send("own_down", (1,))
             send("w_core0")
+            arrived("far_up", (0,))
+            send("far_across", (0,))
+            arrived("far_down", (0,))
+            send("far_across", (2,))
+            arrived("own_across")
+            send("side_up")
+            send("side_down")
+
+        @functools.partial(when, j, 2)
+        def _():
+            arrived("far_up", (1,))
+            send("far_across", (1,))
+            arrived("far_down", (1,))
+            send("far_across", (3,))
+            arrived("w_zup", (0, 1))
+            send("w_fwd_up")
+            arrived("w_zdown", (2, 3))
+            send("w_fwd_down")
+
+        @functools.partial(when, j, 3)
+        def _():
             arrived("own_up", (2, 3))
             send("rest_m")
             arrived("own_down", (0, 1))
             send("rest_p")
-            arrived("own_across")
-            send("side_up")
-            send("side_down")
-
-        @functools.partial(when, j, 2)
-        def _():
-            arrived("far_up", (0,))
-            send("far_across", (0,))
-            arrived("far_down", (0,))
-            send("far_across", (2,))
-            arrived("w_zup", (0, 1))
-            send("w_fwd_up")
-            arrived("w_zdown", (2, 3))
-            send("w_fwd_down")
-
-        @functools.partial(when, j, 3)
-        def _():
-            arrived("far_up", (1,))
-            send("far_across", (1,))
-            arrived("far_down", (1,))
-            send("far_across", (3,))
-
-        @functools.partial(when, j, 4)
-        def _():
-            send("att_own")
             arrived("w_zup", (2, 3))
             send("w_core3")
             arrived("w_zdown", (0, 1))
@@ -366,13 +375,11 @@
 
         @functools.partial(when, j, 6)
         def _():
-            send("att_far")
             arrived("rest_m")
             arrived("side_up")
 
         @functools.partial(when, j, 7)
         def _():
-            send("att_near_m")
             for name in ("w_core0", "w_core3", "w_core1", "w_core2"):
                 arrived(name)
             arrived("att_far")
@@ -387,7 +394,10 @@
         before(j)
         norm(j)
         project()
-        attend(j, t)
+        for half in range(2):
+            attend(j, t, half)
+            for slot, name in ((5, "att_far"), (6, "att_near_m"), (7, "att_near_p")):
+                when(j, slot, functools.partial(send, name, (half,)))
 
         @pl.when(dx == 0)
         def _():
@@ -403,13 +413,13 @@
     load_kv.wait()
     lax.fori_loop(0, 8, step, 0)
 
-    send("att_near_p")
+    send("att_own")
     arrived("att_near_m")
     second(NEAR_M, 3, (2, 3, 0, 1), ("half_down", (0, 1)), "sum_down")
+    arrived("att_near_p")
+    second(NEAR_P, 1, (0, 1, 2, 3), ("half_up", (2, 3)), "sum_up")
     arrived("att_own")
     second(OWN, 0, range(NQ), None, None)
-    arrived("att_near_p")
-    second(NEAR_P, 1, (0, 1, 2, 3), ("half_up", (2, 3)), "sum_up")
 
     restore = powers(me, 1)
     outs = []
@@ -452,7 +462,7 @@
         jnp.asarray(np.concatenate([cosine, cosine], 1), F32),
         jnp.asarray(np.concatenate([-sine, sine], 1), F32),
         jnp.asarray(spread, BF16),
-        jnp.asarray(spread.T, BF16),
+        jnp.asarray(spread.T[: ROWS_B // 2, : PADDED // 2], BF16),
         jnp.asarray(keys, BF16),
         jnp.asarray(values, BF16),
         jnp.asarray(np.stack([even, ~even]), BF16),
@@ -487,7 +497,6 @@
             pltpu.VMEM((SPREAD, HD), BF16),
             pltpu.VMEM((SPREAD, HD), BF16),
             pltpu.VMEM((PADDED, QC), BF16),
-            pltpu.VMEM((ROWS_B, D), BF16),
             pltpu.VMEM((8 * ROWS_B, HD), F32),
             pltpu.VMEM((16, D), F32),
             pltpu.SemaphoreType.DMA((6,)),

time: 135 us -> 133 us (0.985)
  Pallas kernels: 132 us -> 130 us
    pallas_call x1, Pallas kernels: 132 us -> 130 us  [on_device(): pl.pallas_call(body, out_shape=jax.ShapeDtypeStruct(tokens.shape, BF16),...]
where the time goes in v3:
time: 133 us
  Pallas kernels  130 us (98%)
  local copies, waits for them, and re-layouts  2.49 us (2%)
    pallas_call x1, Pallas kernels, on_device(): pl.pallas_call(body, out_shape=jax.ShapeDtypeStruct(tokens.shape, BF16),...  130 us

profile of v3, /device:TPU:0, one launch (start us, length us, event | category | flops | bytes accessed | tf_op | source)
XLA Modules:
  0.0 132.8 jit_solution(2085019468953961091)
XLA Ops:
  0.0 130.2 %verify_block.1 = bf16[160,4096]{1,0:T(8,128)(2,1)} custom-call(bf16[160,4096]{1,0:T(8,128)(2,1)} %tokens_hbm.1, bf16[32,128]{1,0:T(8,128)(2,1)} %bitcast.5, bf16[4096,1024]{1,0:T(8,128)(2,1)} %wq_hbm.1, bf16[4096,128]{1,0:T(8,128)(2,1)} %wk_hbm.1, bf16[4096,128]{1,0:T(8,128)(2,1)} %wv_hbm.1, bf16[1024,4096]{1,0:T(8,128)(2,1)} %wo_hbm.1, ...), custom_call_target="tpu_custom_call" | custom-call | tf_op jit(solution)/shard_map/verify_block/pallas_call | solution.py:479
  130.3 2.5 %copy.17 = bf16[160,4096]{1,0:T(8,128)(2,1)} copy(bf16[160,4096]{1,0:T(8,128)(2,1)} %verify_block.1) | data formatting | bytes 2621440

commit v4 on v3

--- a/solution.py
+++ b/solution.py
@@ -27,7 +27,7 @@
 BF16 = jnp.bfloat16
 SCORE = float(np.log2(np.e) / np.sqrt(HD))
 
-SLOTS = ((0, 0), (1, 0), (0, 2), (0, 3), (0, 1), (1, 2), (1, 3), (1, 1))
+SLOTS = ((0, 0), (0, 2), (0, 3), (1, 2), (0, 1), (1, 3), (1, 1), (1, 0))
 DX_BITS = sum(dx << j for j, (dx, _) in enumerate(SLOTS))
 DY_BITS = sum(dy << (2 * j) for j, (_, dy) in enumerate(SLOTS))
 
@@ -36,24 +36,20 @@
 R_HALF, R_P, R_M = range(3)
 
 QUARTERS = [(q * CH, CH) for q in range(NQ)]
-SIDE = [(0, 1024), (1024, 1024), (2048, 1024), (3072, 512)]
-REST = [(3584, 512)]
 HALVES = [(0, 80), (80, 80)]
 ROUTES = {
-    "own_up": (UP, "x", 0, "x", 3, QUARTERS),
+    "own_up": (UP, "x", 0, "x", 2, QUARTERS),
     "own_down": (DOWN, "x", 0, "x", 4, QUARTERS),
-    "own_across": (ACROSS, "x", 0, "x", 1, QUARTERS),
-    "far_up": (UP, "x", 3, "x", 2, QUARTERS[:2]),
-    "far_down": (DOWN, "x", 4, "x", 2, QUARTERS[2:]),
-    "far_across": (ACROSS, "x", 2, "x", 5, QUARTERS),
-    "side_up": (UP, "x", 1, "x", 6, SIDE),
-    "side_down": (DOWN, "x", 1, "x", 7, SIDE),
-    "rest_m": (ACROSS, "x", 3, "x", 6, REST),
-    "rest_p": (ACROSS, "x", 4, "x", 7, REST),
-    "att_own": (ACROSS, "a", 1, "b", OWN, HALVES),
-    "att_far": (ACROSS, "a", 5, "b", FAR, HALVES),
-    "att_near_m": (ACROSS, "a", 6, "b", NEAR_M, HALVES),
-    "att_near_p": (ACROSS, "a", 7, "b", NEAR_P, HALVES),
+    "own_across": (ACROSS, "x", 0, "x", 7, QUARTERS),
+    "far_up": (UP, "x", 2, "x", 1, QUARTERS[:2]),
+    "far_down": (DOWN, "x", 4, "x", 1, QUARTERS[2:]),
+    "far_across": (ACROSS, "x", 1, "x", 3, QUARTERS),
+    "side_up": (UP, "x", 7, "x", 5, QUARTERS),
+    "side_down": (DOWN, "x", 7, "x", 6, QUARTERS),
+    "att_own": (ACROSS, "a", 7, "b", OWN, HALVES),
+    "att_far": (ACROSS, "a", 3, "b", FAR, HALVES),
+    "att_near_m": (ACROSS, "a", 5, "b", NEAR_M, HALVES),
+    "att_near_p": (ACROSS, "a", 6, "b", NEAR_P, HALVES),
     "half_down": (DOWN, "p", FAR, "r", R_HALF, QUARTERS[:2]),
     "half_up": (UP, "p", FAR, "r", R_HALF, QUARTERS[2:]),
     "sum_down": (DOWN, "p", NEAR_M, "r", R_P, QUARTERS),
@@ -83,12 +79,12 @@
 
 
 def body(
-    tokens_hbm, gain_ref, wq_hbm, wk_hbm, wv_hbm, wo_hbm, kv_hbm, exps_ref, cos_ref, sin_ref,
-    pad_ref, unpad_ref, pad_k_ref, pad_v_ref, parity_ref, out_hbm,
-    xg, pb, rb, ab, bb, w_in, w_out, w_two, kv, xn, qkv, qp, kp, vp, ap, exps, gains,
+    tokens_hbm, gain_hbm, wq_hbm, wk_hbm, wv_hbm, wo_hbm, kv_hbm, exps_hbm, cos_hbm, sin_hbm,
+    pad_hbm, unpad_hbm, pad_k_hbm, pad_v_hbm, parity_hbm, out_hbm,
+    xg, pb, rb, ab, bb, w_in, w_out, w_two, kv, raw, acc, qkv, qp, kp, vp, ap, exps, gains,
+    gain_ref, exps_ref, cos_ref, sin_ref, pad_ref, unpad_ref, pad_k_ref, pad_v_ref, parity_ref,
     load_sem, send_sem, recv_sem, out_sem,
 ):
-    obuf = xn
     me = lax.axis_index("tensor")
     mx, my = me // 4, me % 4
     dp = lax.axis_index("dp")
@@ -158,71 +154,108 @@
             recv_sem=recv_sem.at[k], device_id=targets[target], device_id_type=MESH,
         )
 
-    load_x = pltpu.make_async_copy(tokens_hbm, xg.at[0], load_sem.at[0])
+    def norm():
+        def some(i5, c):
+            squares = []
+            for i in range(5):
+                rows = pl.ds(pl.multiple_of((i5 * 5 + i) * 16, 16), 16)
+                total = None
+                for g in range(D // HD):
+                    x = raw[rows, g * HD : (g + 1) * HD].astype(F32)
+                    total = x * x if g == 0 else total + x * x
+                squares.append(total)
+            scales = [
+                lax.rsqrt(jnp.sum(x, axis=-1, keepdims=True) * (1.0 / D) + EPS) for x in squares
+            ]
+            for i in range(5):
+                rows = pl.ds(pl.multiple_of((i5 * 5 + i) * 16, 16), 16)
+                xg[0, rows, :] = (raw[rows, :].astype(F32) * scales[i] * gains[...]).astype(BF16)
+            return c
+
+        lax.fori_loop(0, 2, some, 0)
+
+    barrier = pltpu.get_barrier_semaphore()
+    for target in targets.values():
+        pl.semaphore_signal(barrier, inc=1, device_id=target, device_id_type=MESH)
+    load_x = pltpu.make_async_copy(tokens_hbm, raw, load_sem.at[0])
     load_o = pltpu.make_async_copy(wo_hbm, w_out, load_sem.at[1])
     load_q = pltpu.make_async_copy(wq_hbm, w_in.at[:, pl.ds(0, QC)], load_sem.at[2])
     load_k = pltpu.make_async_copy(wk_hbm, w_in.at[:, pl.ds(QC, HD)], load_sem.at[3])
     load_v = pltpu.make_async_copy(wv_hbm, w_in.at[:, pl.ds(QC + HD, HD)], load_sem.at[4])
     load_kv = pltpu.make_async_copy(kv_hbm, kv, load_sem.at[5])
-    for copy in (load_x, load_o, load_q, load_k, load_v, load_kv):
+    small = [
+        pltpu.make_async_copy(src, dst, load_sem.at[6 + i])
+        for i, (src, dst) in enumerate((
+            (gain_hbm, gain_ref), (exps_hbm, exps_ref), (cos_hbm, cos_ref), (sin_hbm, sin_ref),
+            (pad_hbm, pad_ref), (unpad_hbm, unpad_ref), (pad_k_hbm, pad_k_ref),
+            (pad_v_hbm, pad_v_ref), (parity_hbm, parity_ref),
+        ))
+    ]
+    for copy in (small[0], load_x, load_o, *small[1:], load_q, load_k, load_v, load_kv):
         copy.start()
-
-    barrier = pltpu.get_barrier_semaphore()
-    for target in targets.values():
-        pl.semaphore_signal(barrier, inc=1, device_id=target, device_id_type=MESH)
+    small[0].wait()
+    gain = gain_ref[...].astype(F32)
+    for g in range(D // HD):
+        gains[:, g * HD : (g + 1) * HD] = jnp.broadcast_to(gain[g : g + 1], (16, HD))
+    load_x.wait()
+    norm()
     pl.semaphore_wait(barrier, len(targets))
 
-    load_x.wait()
     for i in range(NQ):
         if i < 2:
             send("own_up", (i,))
             send("own_down", (i + 2,))
-        send("own_across", (i,))
+        if i < 3:
+            send("own_across", (i,))
     load_o.wait()
     send("w_beyond")
 
-    gain = gain_ref[...].astype(F32)
-    for g in range(D // HD):
-        gains[:, g * HD : (g + 1) * HD] = jnp.broadcast_to(gain[g : g + 1], (16, HD))
+    for copy in small[1:]:
+        copy.wait()
     fill = jnp.zeros((HD - 32, HD), F32)
     for i in range(8 * ROWS_B // HD):
         at = slice(i * HD, (i + 1) * HD)
         exps[at, :] = jnp.concatenate([exps_ref[:, at].astype(F32), fill], 0).T
 
-    def norm(j):
-        def some(i5, c):
-            scales = []
-            for i in range(5):
-                rows = pl.ds(pl.multiple_of((i5 * 5 + i) * 16, 16), 16)
-                squares = None
-                for g in range(D // HD):
-                    x = xg[j, rows, g * HD : (g + 1) * HD].astype(F32)
-                    squares = x * x if g == 0 else squares + x * x
-                scales.append(squares)
-            scales = [lax.rsqrt(jnp.sum(s, axis=-1, keepdims=True) * (1.0 / D) + EPS) for s in scales]
-            for i in range(5):
-                rows = pl.ds(pl.multiple_of((i5 * 5 + i) * 16, 16), 16)
-                xn[rows, :] = (xg[j, rows, :].astype(F32) * scales[i] * gains[...]).astype(BF16)
-            return c
-
-        lax.fori_loop(0, 2, some, 0)
-
     def rot(m):
         return m * cos_ref[...] + pltpu.roll(m, HD // 2, 1) * sin_ref[...]
 
-    def project():
+    def turn(m, n):
+        second_head = rot(m[:, HD:]) if n < 4 else m[:, HD:]
+        return jnp.concatenate([rot(m[:, :HD]), second_head], 1).astype(BF16)
+
+    def project(j):
         for n in range(5):
             at = slice(n * 256, (n + 1) * 256)
-            m = jnp.dot(xn[...], w_in[:, at], preferred_element_type=F32)
-            second = rot(m[:, HD:]) if n < 4 else m[:, HD:]
-            qkv[:, at] = jnp.concatenate([rot(m[:, :HD]), second], 1).astype(BF16)
+            m = jnp.dot(xg[j], w_in[:, at], preferred_element_type=F32)
+            qkv[0, :, at] = turn(m, n)
+
+    early = 3 * CH
+
+    def project_sides(first):
+        for n in range(5):
+            at = slice(n * 256, (n + 1) * 256)
+            if first:
+                rows = xg[5:7, :, :early].reshape(2 * ROWS_B, early)
+                acc[:, at] = jnp.dot(rows, w_in[:early, at], preferred_element_type=F32)
+            else:
+                rows = xg[5:7, :, early:].reshape(2 * ROWS_B, D - early)
+                m = acc[:, at] + jnp.dot(rows, w_in[early:, at], preferred_element_type=F32)
+                for i in range(2):
+                    qkv[i, :, at] = turn(m[i * ROWS_B : (i + 1) * ROWS_B], n)
+
+    def spread_out(i):
         for n in range(4):
             at = slice(n * 256, (n + 1) * 256)
-            qp[:, at] = jnp.dot(pad_ref[...], qkv[:, at], preferred_element_type=F32).astype(BF16)
+            qp[:, at] = jnp.dot(
+                pad_ref[...], qkv[i, :, at], preferred_element_type=F32
+            ).astype(BF16)
         kp[...] = jnp.dot(
-            pad_k_ref[...], qkv[:, QC : QC + HD], preferred_element_type=F32
+            pad_k_ref[...], qkv[i, :, QC : QC + HD], preferred_element_type=F32
         ).astype(BF16)
-        vp[...] = jnp.dot(pad_v_ref[...], qkv[:, QC + HD :], preferred_element_type=F32).astype(BF16)
+        vp[...] = jnp.dot(
+            pad_v_ref[...], qkv[i, :, QC + HD :], preferred_element_type=F32
+        ).astype(BF16)
 
     def attend(j, t, half):
         lane = lax.broadcasted_iota(jnp.int32, (HD, HD), 1)
@@ -291,7 +324,7 @@
             done(q)
 
     def column_block(j):
-        return j - (j + 7) // 8
+        return j - j // 4
 
     def second(k, dy, order, half, name):
         t = mx * 4 + (my + dy) % 4
@@ -335,68 +368,82 @@
                     arrived("own_down", (3,))
                     send("far_down", (1,))
                     send("own_down", (1,))
-            send("w_core0")
             arrived("far_up", (0,))
             send("far_across", (0,))
             arrived("far_down", (0,))
             send("far_across", (2,))
-            arrived("own_across")
-            send("side_up")
-            send("side_down")
-
-        @functools.partial(when, j, 2)
-        def _():
+            send("w_core0")
+            arrived("own_across", (0, 1, 2))
+            send("side_up", (0, 1, 2))
+            send("side_down", (0, 1, 2))
+            arrived("w_zup", (0, 1))
+            send("w_fwd_up")
+            arrived("w_zdown", (2, 3))
+            send("w_fwd_down")
             arrived("far_up", (1,))
             send("far_across", (1,))
             arrived("far_down", (1,))
             send("far_across", (3,))
-            arrived("w_zup", (0, 1))
-            send("w_fwd_up")
-            arrived("w_zdown", (2, 3))
-            send("w_fwd_down")
-
-        @functools.partial(when, j, 3)
-        def _():
-            arrived("own_up", (2, 3))
-            send("rest_m")
-            arrived("own_down", (0, 1))
-            send("rest_p")
+            send("own_across", (3,))
+
+        @functools.partial(when, j, 2)
+        def _():
             arrived("w_zup", (2, 3))
             send("w_core3")
             arrived("w_zdown", (0, 1))
             send("w_core1")
-
-        @functools.partial(when, j, 5)
+            arrived("own_up", (2, 3))
+
+        @functools.partial(when, j, 3)
         def _():
             arrived("w_fwd_up")
             arrived("w_fwd_down")
             send("w_core2")
             arrived("far_across")
 
-        @functools.partial(when, j, 6)
-        def _():
-            arrived("rest_m")
-            arrived("side_up")
-
-        @functools.partial(when, j, 7)
+        @functools.partial(when, j, 4)
+        def _():
+            arrived("own_down", (0, 1))
+            arrived("own_across", (3,))
+            send("side_up", (3,))
+            send("side_down", (3,))
+
+        @functools.partial(when, j, 5)
         def _():
             for name in ("w_core0", "w_core3", "w_core1", "w_core2"):
                 arrived(name)
             arrived("att_far")
             second(FAR, 2, (0, 2, 1, 3), None, "half")
-            arrived("rest_p")
-            arrived("side_down")
+            arrived("side_up", (0, 1, 2))
+            arrived("side_down", (0, 1, 2))
+            project_sides(True)
+            arrived("side_up", (3,))
+            arrived("side_down", (3,))
+            project_sides(False)
+
+        @functools.partial(when, j, 7)
+        def _():
+            arrived("att_near_m")
+            second(NEAR_M, 3, (2, 3, 0, 1), ("half_down", (0, 1)), "sum_down")
+            arrived("att_near_p")
+            second(NEAR_P, 1, (0, 1, 2, 3), ("half_up", (2, 3)), "sum_up")
 
     def step(j, c):
         dx = (DX_BITS >> j) & 1
         dy = (DY_BITS >> (2 * j)) & 3
         t = ((mx + dx) % 2) * 4 + (my + dy) % 4
         before(j)
-        norm(j)
-        project()
+
+        @pl.when((j < 5) | (j == 7))
+        def _():
+            project(j)
+
+        spread_out(j // 6 - j // 7)
         for half in range(2):
             attend(j, t, half)
-            for slot, name in ((5, "att_far"), (6, "att_near_m"), (7, "att_near_p")):
+            for slot, name in (
+                (3, "att_far"), (5, "att_near_m"), (6, "att_near_p"), (7, "att_own"),
+            ):
                 when(j, slot, functools.partial(send, name, (half,)))
 
         @pl.when(dx == 0)
@@ -413,17 +460,12 @@
     load_kv.wait()
     lax.fori_loop(0, 8, step, 0)
 
-    send("att_own")
-    arrived("att_near_m")
-    second(NEAR_M, 3, (2, 3, 0, 1), ("half_down", (0, 1)), "sum_down")
-    arrived("att_near_p")
-    second(NEAR_P, 1, (0, 1, 2, 3), ("half_up", (2, 3)), "sum_up")
     arrived("att_own")
     second(OWN, 0, range(NQ), None, None)
 
     restore = powers(me, 1)
     outs = []
-    for q in range(NQ):
+    for q in (0, 2, 1, 3):
         arrived("sum_down", (q,))
         arrived("sum_up", (q,))
         for g in range(CH // HD):
@@ -432,10 +474,10 @@
             total = pb[OWN, :, at].astype(F32)
             for r in (R_P, R_M):
                 total = total + rb[r, :, at].astype(F32)
-            mixed = xg[0, :, at].astype(F32) + total * restore[:, group : group + 1]
-            obuf[:, at] = mixed.astype(BF16)
+            mixed = raw[:, at].astype(F32) + total * restore[:, group : group + 1]
+            raw[:, at] = mixed.astype(BF16)
         at = pl.ds(*QUARTERS[q])
-        copy = pltpu.make_async_copy(obuf.at[:, at], out_hbm.at[:, at], out_sem.at[q])
+        copy = pltpu.make_async_copy(raw.at[:, at], out_hbm.at[:, at], out_sem.at[q])
         copy.start()
         outs.append(copy)
     for copy in outs:
@@ -474,12 +516,11 @@
 ):
     seqs = past_cache.shape[0]
     pairs = past_cache.reshape(seqs, 2 * CACHE, HD)
-    vmem = pl.BlockSpec(memory_space=pltpu.VMEM)
     anywhere = pl.BlockSpec(memory_space=pl.ANY)
     return pl.pallas_call(
         body,
         out_shape=jax.ShapeDtypeStruct(tokens.shape, BF16),
-        in_specs=[anywhere, vmem, *[anywhere] * 5, *[vmem] * 8],
+        in_specs=[anywhere] * 15,
         out_specs=anywhere,
         scratch_shapes=[
             pltpu.VMEM((8, ROWS_B, D), BF16),
@@ -492,14 +533,24 @@
             pltpu.VMEM((QC, D), BF16),
             pltpu.VMEM((seqs, 2 * CACHE, HD), BF16),
             pltpu.VMEM((ROWS_B, D), BF16),
-            pltpu.VMEM((ROWS_B, QC + 2 * HD), BF16),
+            pltpu.VMEM((2 * ROWS_B, QC + 2 * HD), F32),
+            pltpu.VMEM((2, ROWS_B, QC + 2 * HD), BF16),
             pltpu.VMEM((PADDED, QC), BF16),
             pltpu.VMEM((SPREAD, HD), BF16),
             pltpu.VMEM((SPREAD, HD), BF16),
             pltpu.VMEM((PADDED, QC), BF16),
             pltpu.VMEM((8 * ROWS_B, HD), F32),
             pltpu.VMEM((16, D), F32),
-            pltpu.SemaphoreType.DMA((6,)),
+            pltpu.VMEM((D // HD, HD), BF16),
+            pltpu.VMEM((D // HD, exponents.shape[0]), jnp.int32),
+            pltpu.VMEM((ROWS_B, HD), F32),
+            pltpu.VMEM((ROWS_B, HD), F32),
+            pltpu.VMEM((PADDED, ROWS_B), BF16),
+            pltpu.VMEM((ROWS_B // 2, PADDED // 2), BF16),
+            pltpu.VMEM((SPREAD, ROWS_B), BF16),
+            pltpu.VMEM((SPREAD, ROWS_B), BF16),
+            pltpu.VMEM((2, 32, HD), BF16),
+            pltpu.SemaphoreType.DMA((15,)),
             pltpu.SemaphoreType.DMA((COUNT,)),
             pltpu.SemaphoreType.DMA((COUNT,)),
             pltpu.SemaphoreType.DMA((NQ,)),

time: 133 us -> 130 us (0.977)
  Pallas kernels: 130 us -> 127 us
    pallas_call x1, Pallas kernels: 130 us -> 127 us  [on_device(): pl.pallas_call(body, out_shape=jax.ShapeDtypeStruct(tokens.shape, BF16),...]
where the time goes in v4:
time: 130 us; the launch traced here: 129 us
  Pallas kernels  127 us (98%)
  local copies, waits for them, and re-layouts  2.49 us (2%)
    pallas_call x1, Pallas kernels, on_device(): pl.pallas_call(body, out_shape=jax.ShapeDtypeStruct(tokens.shape, BF16),...  127 us

profile of v4, /device:TPU:0, one launch (start us, length us, event | category | flops | bytes accessed | tf_op | source)
XLA Modules:
  0.0 129.3 jit_solution(5479014260172804956)
XLA Ops:
  0.0 126.8 %verify_block.1 = bf16[160,4096]{1,0:T(8,128)(2,1)} custom-call(bf16[160,4096]{1,0:T(8,128)(2,1)} %tokens_hbm.1, bf16[32,128]{1,0:T(8,128)(2,1)} %bitcast.5, bf16[4096,1024]{1,0:T(8,128)(2,1)} %wq_hbm.1, bf16[4096,128]{1,0:T(8,128)(2,1)} %wk_hbm.1, bf16[4096,128]{1,0:T(8,128)(2,1)} %wv_hbm.1, bf16[1024,4096]{1,0:T(8,128)(2,1)} %wo_hbm.1, ...), custom_call_target="tpu_custom_call" | custom-call | tf_op jit(solution)/shard_map/verify_block/pallas_call | solution.py:520
  126.8 2.5 %copy.17 = bf16[160,4096]{1,0:T(8,128)(2,1)} copy(bf16[160,4096]{1,0:T(8,128)(2,1)} %verify_block.1) | data formatting | bytes 2621440

commit v5 on v4

--- a/solution.py
+++ b/solution.py
@@ -36,7 +36,9 @@
 R_HALF, R_P, R_M = range(3)
 
 QUARTERS = [(q * CH, CH) for q in range(NQ)]
-HALVES = [(0, 80), (80, 80)]
+HALF = ROWS_B // 2
+HALVES = [(0, HALF), (HALF, HALF)]
+EIGHTHS = [(q * CH, CH, r * HALF, HALF) for r in range(2) for q in range(NQ)]
 ROUTES = {
     "own_up": (UP, "x", 0, "x", 2, QUARTERS),
     "own_down": (DOWN, "x", 0, "x", 4, QUARTERS),
@@ -52,8 +54,8 @@
     "att_near_p": (ACROSS, "a", 6, "b", NEAR_P, HALVES),
     "half_down": (DOWN, "p", FAR, "r", R_HALF, QUARTERS[:2]),
     "half_up": (UP, "p", FAR, "r", R_HALF, QUARTERS[2:]),
-    "sum_down": (DOWN, "p", NEAR_M, "r", R_P, QUARTERS),
-    "sum_up": (UP, "p", NEAR_P, "r", R_M, QUARTERS),
+    "sum_down": (DOWN, "p", NEAR_M, "r", R_P, EIGHTHS),
+    "sum_up": (UP, "p", NEAR_P, "r", R_M, EIGHTHS),
 }
 WEIGHTS = {
     "w_beyond": (BEYOND, True, 0, (0, 1, 2, 3)),
@@ -106,8 +108,11 @@
         k = BASE[name] + i
         if name in ROUTES:
             target, sbuf, sslot, dbuf, dslot, pieces = ROUTES[name]
-            at = pl.ds(*pieces[i])
-            if sbuf == "a":
+            at = pl.ds(*pieces[i][:2])
+            if len(pieces[i]) == 4:
+                rows = pl.ds(*pieces[i][2:])
+                src, dst = buffers[sbuf].at[sslot, rows, at], buffers[dbuf].at[dslot, rows, at]
+            elif sbuf == "a":
                 src, dst = ab.at[sslot, at, :], bb.at[dslot, at, :]
             else:
                 src, dst = buffers[sbuf].at[sslot, :, at], buffers[dbuf].at[dslot, :, at]
@@ -302,14 +307,15 @@
                 unpad_ref[...], padded, preferred_element_type=F32
             ).astype(BF16)
 
-    def powers(t, sign):
-        e = exps[pl.ds(pl.multiple_of(t * ROWS_B, ROWS_B), ROWS_B), :].astype(jnp.int32)
+    def powers(t, sign, first=0, count=ROWS_B):
+        e = exps[pl.ds(pl.multiple_of(t * ROWS_B + first, 16), count), :].astype(jnp.int32)
         if sign < 0:
             return jnp.left_shift(1, -e).astype(F32)
         return jnp.left_shift(1, e + 11).astype(F32) * (2.0**-11)
 
-    def out_project(att, weights, k, t, order, extra, done):
-        shrink = powers(t, -1)
+    def out_project(att, weights, k, t, order, extra, done, first=0, count=ROWS_B):
+        shrink = powers(t, -1, first, count)
+        rows = slice(first, first + count)
         for q in order:
             for base in (q * CH, q * CH + 512):
                 part = jnp.dot(att, weights[:, base : base + 512], preferred_element_type=F32)
@@ -319,31 +325,39 @@
                     scaled = part[:, g * HD : (g + 1) * HD] * shrink[:, group : group + 1]
                     scaled = jnp.clip(scaled, -127.0, 127.0).astype(BF16)
                     for r in extra(q, g == 0 and base == q * CH):
-                        scaled = scaled.astype(F32) + r[:, at].astype(F32)
-                    pb[k, :, at] = scaled.astype(BF16)
+                        scaled = scaled.astype(F32) + r[rows, at].astype(F32)
+                    pb[k, rows, at] = scaled.astype(BF16)
             done(q)
 
     def column_block(j):
         return j - j // 4
 
-    def second(k, dy, order, half, name):
-        t = mx * 4 + (my + dy) % 4
-
-        def extra(q, first):
+    def second(k, dy, order, send_sum, half=None, part=None):
+        first, count = HALVES[part] if part is not None else (0, ROWS_B)
+
+        def extra(q, opening):
             refs = [pb.at[k]]
             if half is not None and q in half[1]:
-                if first:
+                if opening and part == 0:
                     arrived(half[0], (half[1].index(q),))
                 refs.append(rb.at[R_HALF])
             return refs
 
-        def done(q):
-            if name == "half":
-                send("half_down" if q < 2 else "half_up", (q % 2,))
-            elif name:
-                send(name, (q,))
-
-        out_project(bb[k], w_two, k, t, order, extra, done)
+        out_project(
+            bb[k, first : first + count], w_two, k, mx * 4 + (my + dy) % 4, order, extra, send_sum,
+            first, count,
+        )
+
+    def near(up, part, order):
+        name = "sum_up" if up else "sum_down"
+
+        def send_sum(q):
+            send(name, (part * NQ + q,))
+
+        if up:
+            second(NEAR_P, 1, order, send_sum, ("half_up", (2, 3)), part)
+        else:
+            second(NEAR_M, 3, order, send_sum, ("half_down", (0, 1)), part)
 
     def when(j, k, action):
         pl.when(j == k)(action)
@@ -413,7 +427,7 @@
             for name in ("w_core0", "w_core3", "w_core1", "w_core2"):
                 arrived(name)
             arrived("att_far")
-            second(FAR, 2, (0, 2, 1, 3), None, "half")
+            second(FAR, 2, (0, 2, 1, 3), lambda q: send("half_down" if q < 2 else "half_up", (q % 2,)))
             arrived("side_up", (0, 1, 2))
             arrived("side_down", (0, 1, 2))
             project_sides(True)
@@ -423,10 +437,16 @@
 
         @functools.partial(when, j, 7)
         def _():
-            arrived("att_near_m")
-            second(NEAR_M, 3, (2, 3, 0, 1), ("half_down", (0, 1)), "sum_down")
-            arrived("att_near_p")
-            second(NEAR_P, 1, (0, 1, 2, 3), ("half_up", (2, 3)), "sum_up")
+            arrived("att_near_m", (0,))
+            near(False, 0, (2, 3))
+            arrived("att_near_p", (0,))
+            near(True, 0, (0, 1))
+            near(False, 0, (0, 1))
+            near(True, 0, (2, 3))
+            arrived("att_near_m", (1,))
+            near(False, 1, (2, 3, 0, 1))
+            arrived("att_near_p", (1,))
+            near(True, 1, (0, 1, 2, 3))
 
     def step(j, c):
         dx = (DX_BITS >> j) & 1
@@ -441,10 +461,13 @@
         spread_out(j // 6 - j // 7)
         for half in range(2):
             attend(j, t, half)
-            for slot, name in (
-                (3, "att_far"), (5, "att_near_m"), (6, "att_near_p"), (7, "att_own"),
-            ):
-                when(j, slot, functools.partial(send, name, (half,)))
+            when(j, 3, functools.partial(send, "att_far", (half,)))
+            when(j, 7, functools.partial(send, "att_own", (half,)))
+            if half == 0:
+                when(j, 5, functools.partial(send, "att_near_m", (0,)))
+            when(j, 6, functools.partial(send, "att_near_p", (half,)))
+            if half == 0:
+                when(j, 6, functools.partial(send, "att_near_m", (1,)))
 
         @pl.when(dx == 0)
         def _():
@@ -461,25 +484,27 @@
     lax.fori_loop(0, 8, step, 0)
 
     arrived("att_own")
-    second(OWN, 0, range(NQ), None, None)
+    second(OWN, 0, range(NQ), lambda q: None)
 
     restore = powers(me, 1)
     outs = []
-    for q in (0, 2, 1, 3):
-        arrived("sum_down", (q,))
-        arrived("sum_up", (q,))
-        for g in range(CH // HD):
-            group = q * (CH // HD) + g
-            at = slice(group * HD, (group + 1) * HD)
-            total = pb[OWN, :, at].astype(F32)
-            for r in (R_P, R_M):
-                total = total + rb[r, :, at].astype(F32)
-            mixed = raw[:, at].astype(F32) + total * restore[:, group : group + 1]
-            raw[:, at] = mixed.astype(BF16)
-        at = pl.ds(*QUARTERS[q])
-        copy = pltpu.make_async_copy(raw.at[:, at], out_hbm.at[:, at], out_sem.at[q])
-        copy.start()
-        outs.append(copy)
+    for part in range(2):
+        rows = slice(part * HALF, (part + 1) * HALF)
+        for q in (0, 2, 1, 3):
+            arrived("sum_down", (part * NQ + q,))
+            arrived("sum_up", (part * NQ + q,))
+            for g in range(CH // HD):
+                group = q * (CH // HD) + g
+                at = slice(group * HD, (group + 1) * HD)
+                total = pb[OWN, rows, at].astype(F32)
+                for r in (R_P, R_M):
+                    total = total + rb[r, rows, at].astype(F32)
+                mixed = raw[rows, at].astype(F32) + total * restore[rows, group : group + 1]
+                raw[rows, at] = mixed.astype(BF16)
+            tile = (pl.ds(*HALVES[part]), pl.ds(*QUARTERS[q]))
+            copy = pltpu.make_async_copy(raw.at[tile], out_hbm.at[tile], out_sem.at[part * NQ + q])
+            copy.start()
+            outs.append(copy)
     for copy in outs:
         copy.wait()
     for name in (*ROUTES, *WEIGHTS):
@@ -553,7 +578,7 @@
             pltpu.SemaphoreType.DMA((15,)),
             pltpu.SemaphoreType.DMA((COUNT,)),
             pltpu.SemaphoreType.DMA((COUNT,)),
-            pltpu.SemaphoreType.DMA((NQ,)),
+            pltpu.SemaphoreType.DMA((2 * NQ,)),
         ],
         compiler_params=pltpu.CompilerParams(
             collective_id=0, has_side_effects=True, vmem_limit_bytes=67_000_000

time: 130 us -> 126 us (0.969)
  Pallas kernels: 127 us -> 123 us
    pallas_call x1, Pallas kernels: 127 us -> 123 us  [on_device(): pl.pallas_call(body, out_shape=jax.ShapeDtypeStruct(tokens.shape, BF16),...]
where the time goes in v5:
time: 126 us; the launch traced here: 125 us
  Pallas kernels  123 us (98%)
  local copies, waits for them, and re-layouts  2.49 us (2%)
    pallas_call x1, Pallas kernels, on_device(): pl.pallas_call(body, out_shape=jax.ShapeDtypeStruct(tokens.shape, BF16),...  123 us

profile of v5, /device:TPU:0, one launch (start us, length us, event | category | flops | bytes accessed | tf_op | source)
XLA Modules:
  0.0 125.3 jit_solution(9428180571437360487)
XLA Ops:
  0.0 122.8 %verify_block.1 = bf16[160,4096]{1,0:T(8,128)(2,1)} custom-call(bf16[160,4096]{1,0:T(8,128)(2,1)} %tokens_hbm.1, bf16[32,128]{1,0:T(8,128)(2,1)} %bitcast.5, bf16[4096,1024]{1,0:T(8,128)(2,1)} %wq_hbm.1, bf16[4096,128]{1,0:T(8,128)(2,1)} %wk_hbm.1, bf16[4096,128]{1,0:T(8,128)(2,1)} %wv_hbm.1, bf16[1024,4096]{1,0:T(8,128)(2,1)} %wo_hbm.1, ...), custom_call_target="tpu_custom_call" | custom-call | tf_op jit(solution)/shard_map/verify_block/pallas_call | solution.py:545
  122.8 2.5 %copy.17 = bf16[160,4096]{1,0:T(8,128)(2,1)} copy(bf16[160,4096]{1,0:T(8,128)(2,1)} %verify_block.1) | data formatting | bytes 2621440

commit v6 on v5

--- a/solution.py
+++ b/solution.py
@@ -82,10 +82,10 @@
 
 def body(
     tokens_hbm, gain_hbm, wq_hbm, wk_hbm, wv_hbm, wo_hbm, kv_hbm, exps_hbm, cos_hbm, sin_hbm,
-    pad_hbm, unpad_hbm, pad_k_hbm, pad_v_hbm, parity_hbm, out_hbm,
-    xg, pb, rb, ab, bb, w_in, w_out, w_two, kv, raw, acc, qkv, qp, kp, vp, ap, exps, gains,
+    pad_hbm, unpad_hbm, pad_k_hbm, pad_v_hbm, parity_hbm, raw,
+    xg, pb, rb, ab, bb, w_in, w_out, w_two, kv, acc, qkv, qp, kp, vp, ap, exps, gains,
     gain_ref, exps_ref, cos_ref, sin_ref, pad_ref, unpad_ref, pad_k_ref, pad_v_ref, parity_ref,
-    load_sem, send_sem, recv_sem, out_sem,
+    load_sem, send_sem, recv_sem,
 ):
     me = lax.axis_index("tensor")
     mx, my = me // 4, me % 4
@@ -487,7 +487,6 @@
     second(OWN, 0, range(NQ), lambda q: None)
 
     restore = powers(me, 1)
-    outs = []
     for part in range(2):
         rows = slice(part * HALF, (part + 1) * HALF)
         for q in (0, 2, 1, 3):
@@ -501,12 +500,6 @@
                     total = total + rb[r, rows, at].astype(F32)
                 mixed = raw[rows, at].astype(F32) + total * restore[rows, group : group + 1]
                 raw[rows, at] = mixed.astype(BF16)
-            tile = (pl.ds(*HALVES[part]), pl.ds(*QUARTERS[q]))
-            copy = pltpu.make_async_copy(raw.at[tile], out_hbm.at[tile], out_sem.at[part * NQ + q])
-            copy.start()
-            outs.append(copy)
-    for copy in outs:
-        copy.wait()
     for name in (*ROUTES, *WEIGHTS):
         for i in pieces_of(name, None):
             route(name, i).wait_send()
@@ -544,9 +537,9 @@
     anywhere = pl.BlockSpec(memory_space=pl.ANY)
     return pl.pallas_call(
         body,
-        out_shape=jax.ShapeDtypeStruct(tokens.shape, BF16),
+        out_shape=pltpu.VMEM(tokens.shape, BF16),
         in_specs=[anywhere] * 15,
-        out_specs=anywhere,
+        out_specs=pl.BlockSpec(memory_space=pltpu.VMEM),
         scratch_shapes=[
             pltpu.VMEM((8, ROWS_B, D), BF16),
             pltpu.VMEM((4, ROWS_B, D), BF16),
@@ -557,7 +550,6 @@
             pltpu.VMEM((QC, D), BF16),
             pltpu.VMEM((QC, D), BF16),
             pltpu.VMEM((seqs, 2 * CACHE, HD), BF16),
-            pltpu.VMEM((ROWS_B, D), BF16),
             pltpu.VMEM((2 * ROWS_B, QC + 2 * HD), F32),
             pltpu.VMEM((2, ROWS_B, QC + 2 * HD), BF16),
             pltpu.VMEM((PADDED, QC), BF16),
@@ -578,10 +570,9 @@
             pltpu.SemaphoreType.DMA((15,)),
             pltpu.SemaphoreType.DMA((COUNT,)),
             pltpu.SemaphoreType.DMA((COUNT,)),
-            pltpu.SemaphoreType.DMA((2 * NQ,)),
         ],
         compiler_params=pltpu.CompilerParams(
-            collective_id=0, has_side_effects=True, vmem_limit_bytes=67_000_000
+            collective_id=0, has_side_effects=True, vmem_limit_bytes=64_000_000
         ),
         name="verify_block",
     )(

time: 126 us -> 124 us (0.984)
  local copies, waits for them, and re-layouts: 2.49 us -> 1.06 us
    unnamed x1, local copies, waits for them, and re-layouts: 2.49 us -> 1.06 us
where the time goes in v6:
time: 124 us; the launch traced here: 123 us
  Pallas kernels  122 us (98%)
    pallas_call x1, Pallas kernels, on_device(): pl.pallas_call(body, out_shape=pltpu.VMEM(tokens.shape, BF16), in_specs=[...  122 us

profile of v6, /device:TPU:0, one launch (start us, length us, event | category | flops | bytes accessed | tf_op | source)
XLA Modules:
  0.0 123.1 jit_solution(3730084994360216211)
XLA Ops:
  0.0 122.0 %verify_block.1 = bf16[160,4096]{1,0:T(8,128)(2,1)S(1)} custom-call(bf16[160,4096]{1,0:T(8,128)(2,1)} %tokens_hbm.1, bf16[32,128]{1,0:T(8,128)(2,1)} %bitcast.5, bf16[4096,1024]{1,0:T(8,128)(2,1)} %wq_hbm.1, bf16[4096,128]{1,0:T(8,128)(2,1)} %wk_hbm.1, bf16[4096,128]{1,0:T(8,128)(2,1)} %wv_hbm.1, bf16[1024,4096]{1,0:T(8,128)(2,1)} %wo_hbm.1, ...), custom_call_target="tpu_custom_call" | custom-call | tf_op jit(solution)/shard_map/verify_block/pallas_call | solution.py:538
  122.0 1.1 copy.17

commit v7 on v6

--- a/solution.py
+++ b/solution.py
@@ -486,6 +486,11 @@
     arrived("att_own")
     second(OWN, 0, range(NQ), lambda q: None)
 
+    last = ("sum_down", "sum_up")
+    for name in (*ROUTES, *WEIGHTS):
+        if name not in last:
+            for i in pieces_of(name, None):
+                route(name, i).wait_send()
     restore = powers(me, 1)
     for part in range(2):
         rows = slice(part * HALF, (part + 1) * HALF)
@@ -500,7 +505,7 @@
                     total = total + rb[r, rows, at].astype(F32)
                 mixed = raw[rows, at].astype(F32) + total * restore[rows, group : group + 1]
                 raw[rows, at] = mixed.astype(BF16)
-    for name in (*ROUTES, *WEIGHTS):
+    for name in last:
         for i in pieces_of(name, None):
             route(name, i).wait_send()
 

time: 124 us -> 124 us (level)
  no operation moved by 1% of the time
where the time goes in v7:
time: 124 us; the launch traced here: 123 us
  Pallas kernels  122 us (98%)
    pallas_call x1, Pallas kernels, on_device(): pl.pallas_call(body, out_shape=pltpu.VMEM(tokens.shape, BF16), in_specs=[...  122 us

profile of v7, /device:TPU:0, one launch (start us, length us, event | category | flops | bytes accessed | tf_op | source)
XLA Modules:
  0.0 123.0 jit_solution(17850897889620117463)
XLA Ops:
  0.0 121.9 %verify_block.1 = bf16[160,4096]{1,0:T(8,128)(2,1)S(1)} custom-call(bf16[160,4096]{1,0:T(8,128)(2,1)} %tokens_hbm.1, bf16[32,128]{1,0:T(8,128)(2,1)} %bitcast.5, bf16[4096,1024]{1,0:T(8,128)(2,1)} %wq_hbm.1, bf16[4096,128]{1,0:T(8,128)(2,1)} %wk_hbm.1, bf16[4096,128]{1,0:T(8,128)(2,1)} %wv_hbm.1, bf16[1024,4096]{1,0:T(8,128)(2,1)} %wo_hbm.1, ...), custom_call_target="tpu_custom_call" | custom-call | tf_op jit(solution)/shard_map/verify_block/pallas_call | solution.py:543
  122.0 1.1 copy.17
